TPU v7x, 32 devices: a whole 2x2x4 slice. The times are simulated.
32 devices in a mesh: groups: 2 (over x), head: 8 (over z, y), batch: 2 (over core).
Axes of the slice: x: 2, y: 2, z: 4, core: 2. Of those that a mesh axis runs over, the one named last changes fastest.
Arguments:
- latent_rows: bfloat16 [4096, 576], P(('groups', 'batch', 'head')), parts along dimension 0, may hold values from -6 to 6
- pre_queries: bfloat16 [4096, 128, 192], P(('groups', 'batch'), 'head'), parts along dimension 0, may hold values from -270 to 270
- pre_lengths: int32 [4, 4], P('groups'), parts along dimension 0, may hold values from 1 to 512, 1024 in all within a row
- owner_map: int32 [4, 4], P('groups'), parts along dimension 0, may hold values from 0 to 31, as said below
- context_cache: bfloat16 [64, 4096, 576], P(('groups', 'batch', 'head')), parts along dimension 0, may hold values from -6 to 6
- context_lengths: int32 [64], P(('groups', 'batch', 'head')), parts along dimension 0, may hold values from 1 to 4096, 65536 in all
- new_latent: bfloat16 [4, 32, 576], P('groups', ('batch', 'head')), parts along dimension 0, may hold values from -6 to 6
- dec_queries: bfloat16 [4, 32, 128, 192], P('groups', 'batch', 'head'), parts along dimension 0, may hold values from -270 to 270
- key_weight: bfloat16 [512, 16384], P(None, 'head'), may hold values from -0.25 to 0.25
- value_weight: bfloat16 [512, 16384], P(None, 'head'), may hold values from -0.25 to 0.25
Outputs:
- prefill_out: bfloat16 [4096, 16384], P(('groups', 'batch'), 'head'), parts along dimension 0
- decode_out: bfloat16 [4, 32, 16384], P('groups', 'batch', 'head'), parts along dimension 0
There are 2 independent parts, one for each index of `groups`. A program takes and returns all parts, laid end to end along the dimension named above; an argument that names none is the same for every part. Nothing has to cross between parts.
Inputs may be any that keep to these rules, and one draw needn't show every extreme that they name: `owner_map`: the entries are distinct decode requests.
All inputs are finite; a program needn't handle non-finite values. No bound on the sum of `context_lengths` on one device may be relied on, other than what follows from the above.
Results may differ from a plain program's by a relative error of at most 0.0061.
Values may be sent and summed in bfloat16 or wider, within the bound.
A program may use at most 192 MiB of HBM per device.

v0:
```python
import functools
import math

import jax
import jax.numpy as jnp
from jax import lax
from jax.experimental import pallas as pl
from jax.experimental.pallas import tpu as pltpu
from jax.sharding import PartitionSpec as P

BLK = 512


NEGATIVE = -1e30


def from_partner(value, axis, distance):
    mask = 2**distance
    pairs = [(source, source ^ mask) for source in range(lax.axis_size(axis))]
    return lax.ppermute(value, axis, pairs)


def request_table(pre_lengths, owner_map, span_len):
    seg_ends = jnp.cumsum(pre_lengths, axis=1)
    span_base = jnp.arange(pre_lengths.shape[0], dtype=jnp.int32)[:, None] * span_len
    seg_starts = seg_ends - pre_lengths + span_base
    return (owner_map.reshape(-1), seg_starts.reshape(-1), pre_lengths.reshape(-1))


def prefill_heads(own_span, queries, span_lengths, key_weight, value_weight):
    span_len, head_count, query_width = queries.shape
    head_size = key_weight.shape[1] // head_count
    lat_width = key_weight.shape[0]
    score_scale = 1.0 / math.sqrt(query_width)
    latent = own_span[:, :lat_width]
    rope_keys = own_span[:, lat_width:]
    keys_nope = (
        jnp.dot(latent, key_weight, preferred_element_type=jnp.float32)
        .astype(jnp.bfloat16)
        .reshape(span_len, head_count, head_size)
    )
    values = (
        jnp.dot(latent, value_weight, preferred_element_type=jnp.float32)
        .astype(jnp.bfloat16)
        .reshape(span_len, head_count, head_size)
    )
    scores = jnp.einsum(
        "qhd,khd->hqk", queries[:, :, :head_size], keys_nope, preferred_element_type=jnp.float32
    )
    scores = scores + jnp.einsum(
        "qhr,kr->hqk", queries[:, :, head_size:], rope_keys, preferred_element_type=jnp.float32
    )
    scores = scores * score_scale
    seg_ends = jnp.cumsum(span_lengths)
    places = jnp.arange(span_len, dtype=jnp.int32)
    segment = jnp.sum((places[:, None] >= seg_ends[None, :]).astype(jnp.int32), axis=1)
    allowed = (segment[:, None] == segment[None, :]) & (places[None, :] <= places[:, None])
    masked = jnp.where(allowed[None], scores, NEGATIVE)
    peak_score = jnp.max(masked, axis=2, keepdims=True)
    weights = jnp.exp(masked - peak_score)
    weight_sum = jnp.sum(weights, axis=2)
    mixed_out = jnp.einsum(
        "hqk,khd->qhd", weights.astype(jnp.bfloat16), values, preferred_element_type=jnp.float32
    )
    mixed_out = mixed_out / jnp.transpose(weight_sum)[:, :, None]
    return mixed_out.astype(jnp.bfloat16).reshape(span_len, head_count * head_size)


def plain_on_device(
    latent_rows,
    pre_queries,
    pre_lengths,
    owner_map,
    context_cache,
    context_lengths,
    new_latent,
    dec_queries,
    key_weight,
    value_weight,
):
    head_rank = lax.axis_index("head")
    batch_rank = lax.axis_index("batch")
    span_len = pre_queries.shape[0]
    kv_width = latent_rows.shape[1]
    own_span = lax.all_gather(latent_rows, "head", axis=0, tiled=True)
    other_span = from_partner(own_span, "batch", 0)
    first_span = jnp.where(batch_rank == 0, own_span, other_span)
    second_span = jnp.where(batch_rank == 0, other_span, own_span)
    all_spans = jnp.concatenate([first_span, second_span], axis=0)
    span_lengths = lax.dynamic_index_in_dim(pre_lengths, batch_rank, 0, keepdims=False)
    prefill_out = prefill_heads(own_span, pre_queries, span_lengths, key_weight, value_weight)
    step_total, rows_local, head_count, query_width = dec_queries.shape
    lat_width = key_weight.shape[0]
    head_size = key_weight.shape[1] // head_count
    owned_rows = context_cache.shape[0]
    score_scale = 1.0 / math.sqrt(query_width)
    key_heads = key_weight.reshape(lat_width, head_count, head_size)
    value_heads = value_weight.reshape(lat_width, head_count, head_size)
    absorbed = jnp.einsum(
        "srhd,lhd->srhl",
        dec_queries[..., :head_size],
        key_heads,
        preferred_element_type=jnp.float32,
    ).astype(jnp.bfloat16)
    query_all = jnp.concatenate([absorbed, dec_queries[..., head_size:]], axis=3)
    flat_owner, flat_start, flat_length = request_table(pre_lengths, owner_map, span_len)
    row_ids = (
        batch_rank * rows_local + head_rank * owned_rows + jnp.arange(owned_rows, dtype=jnp.int32)
    )
    matches = (flat_owner[None, :] == row_ids[:, None]).astype(jnp.int32)
    is_target = jnp.sum(matches, axis=1) > 0
    first_row = jnp.sum(matches * flat_start[None, :], axis=1)
    prompt_len = jnp.sum(matches * flat_length[None, :], axis=1)
    effective = jnp.where(is_target, prompt_len, context_lengths)
    padded = jnp.concatenate([all_spans, jnp.zeros((span_len, kv_width), all_spans.dtype)], axis=0)
    replaced = jax.vmap(lambda offset: lax.dynamic_slice_in_dim(padded, offset, span_len, 0))(
        first_row
    )
    front_rows = jnp.where(is_target[:, None, None], replaced, context_cache[:, :span_len])
    front_blocks = span_len // BLK
    needed = (jnp.max(effective) + BLK - 1) // BLK
    fresh_latent = new_latent[..., :lat_width]
    owned_query = lax.all_to_all(query_all, "head", split_axis=1, concat_axis=2, tiled=True)
    fresh_scores = (
        jnp.einsum("srhk,jrk->srhj", owned_query, new_latent, preferred_element_type=jnp.float32)
        * score_scale
    )
    visible = (
        jnp.arange(new_latent.shape[0], dtype=jnp.int32)[None, :]
        <= jnp.arange(step_total, dtype=jnp.int32)[:, None]
    )
    fresh_scores = jnp.where(visible[:, None, None, :], fresh_scores, NEGATIVE)
    peak_score = jnp.max(fresh_scores, axis=3)
    weights = jnp.exp(fresh_scores - peak_score[..., None])
    weight_sum = jnp.sum(weights, axis=3)
    running = jnp.einsum(
        "srhj,jrl->srhl",
        weights.astype(jnp.bfloat16),
        fresh_latent,
        preferred_element_type=jnp.float32,
    )

    def advance(block_index, state_tuple, source):
        old_peak, old_sum, old_running = state_tuple
        key_block = lax.dynamic_slice_in_dim(source, block_index * BLK, BLK, 1)
        scores = (
            jnp.einsum("srhk,rtk->srht", owned_query, key_block, preferred_element_type=jnp.float32)
            * score_scale
        )
        places = block_index * BLK + jnp.arange(BLK, dtype=jnp.int32)
        in_context = places[None, :] < effective[:, None]
        scores = jnp.where(in_context[None, :, None, :], scores, NEGATIVE)
        new_peak = jnp.maximum(old_peak, jnp.max(scores, axis=3))
        factor = jnp.exp(old_peak - new_peak)
        block_weights = jnp.exp(scores - new_peak[..., None])
        new_sum = old_sum * factor + jnp.sum(block_weights, axis=3)
        new_running = old_running * factor[..., None] + jnp.einsum(
            "srht,rtl->srhl",
            block_weights.astype(jnp.bfloat16),
            key_block[..., :lat_width],
            preferred_element_type=jnp.float32,
        )
        return (new_peak, new_sum, new_running)

    state_tuple = lax.fori_loop(
        0,
        jnp.minimum(needed, front_blocks),
        lambda block_index, state_now: advance(block_index, state_now, front_rows),
        (peak_score, weight_sum, running),
    )
    state_tuple = lax.fori_loop(
        front_blocks,
        jnp.maximum(needed, front_blocks),
        lambda block_index, state_now: advance(block_index, state_now, context_cache),
        state_tuple,
    )
    latent_out = (state_tuple[2] / state_tuple[1][..., None]).astype(jnp.bfloat16)
    returned = lax.all_to_all(latent_out, "head", split_axis=2, concat_axis=1, tiled=True)
    projected = jnp.einsum(
        "srhl,lhd->srhd", returned, value_heads, preferred_element_type=jnp.float32
    ).astype(jnp.bfloat16)
    decode_out = projected.reshape(query_all.shape[0], rows_local, head_count * head_size)
    return (prefill_out, decode_out)


def trans_dot(left, right):
    return lax.dot_general(
        left, right, (((1,), (1,)), ((), ())), preferred_element_type=jnp.float32
    )


def prefill_kernel(
    lens_ref, shards_ref, q_ref, kw_ref, vw_ref, out_ref, bias_ref, keys_ref, vals_ref, latent_ref, *, lat, qb, look, scale
):
    span_len = latent_ref.shape[0]
    own = shards_ref.shape[2]
    pair = keys_ref.shape[0]
    segs = lens_ref.shape[0]
    blocks = span_len // qb
    ends = []
    total = 0
    for k in range(segs):
        total = total + lens_ref[k]
        ends.append(total)

    @pl.when(pl.program_id(0) == 0)
    def _():
        for k in range(span_len // own):
            latent_ref[k * own : (k + 1) * own, :] = jnp.transpose(shards_ref[k])
        for p in range(pair):
            keys_ref[p, :, 128:] = latent_ref[:, lat:]
        width = (look + 1) * qb
        for i in range(blocks):
            rows = i * qb + lax.broadcasted_iota(jnp.int32, (width, qb), 1)
            cols = (i - look) * qb + lax.broadcasted_iota(jnp.int32, (width, qb), 0)
            row_start = jnp.zeros((width, qb), jnp.int32)
            for end in ends:
                row_start = jnp.where(rows >= end, end, row_start)
            seen = (cols >= row_start) & (cols <= rows)
            bias_ref[i] = jnp.where(seen, 0.0, NEGATIVE)

    latent = latent_ref[:, :lat]
    keys = jnp.dot(latent, kw_ref[...], preferred_element_type=jnp.float32).astype(jnp.bfloat16)
    for p in range(pair):
        keys_ref[p, :, :128] = keys[:, p * 128 : (p + 1) * 128]
    vals = jnp.dot(latent, vw_ref[...], preferred_element_type=jnp.float32)
    vals_ref[...] = jnp.transpose(vals.astype(jnp.bfloat16))

    def attend(i, back):
        lo, hi = (i - back) * qb, (i + 1) * qb
        bias = bias_ref[i, (look - back) * qb :, :]
        for p in range(pair):
            s = (
                jnp.dot(
                    keys_ref[p, lo:hi, :],
                    q_ref[p, :, i * qb : hi],
                    preferred_element_type=jnp.float32,
                )
                + bias
            )
            m = jnp.max(s, axis=0, keepdims=True)
            w = jnp.exp2((s - m) * scale)
            l = jnp.sum(w, axis=0, keepdims=True)
            o = jnp.dot(
                vals_ref[p * 128 : (p + 1) * 128, lo:hi],
                w.astype(jnp.bfloat16),
                preferred_element_type=jnp.float32,
            )
            o = jnp.transpose(o / l)
            out_ref[i * qb : hi, p * 128 : (p + 1) * 128] = o.astype(out_ref.dtype)

    for i in range(blocks):
        most = min(i, look)
        if most == 0:
            attend(i, 0)
            continue
        first = jnp.int32(0)
        for end in ends:
            first = jnp.where(i * qb >= end, end, first)
        need = i - first // qb
        for back in range(most + 1):
            pl.when(need == back)(functools.partial(attend, i, back))


def prefill_pallas(own_span, queries, span_lengths, key_weight, value_weight, qb=256):
    span_len, heads, width = queries.shape
    lat = key_weight.shape[0]
    kv = own_span.shape[1]
    shards, _, own = own_span.shape
    most_request = span_len // 2
    look = min(-(-most_request // qb), span_len // qb - 1)
    pair = 2
    scale = math.log2(math.e) / math.sqrt(width)
    q_turned = jnp.transpose(queries, (1, 2, 0))
    return pl.pallas_call(
        functools.partial(prefill_kernel, lat=lat, qb=qb, look=look, scale=scale),
        out_shape=jax.ShapeDtypeStruct((span_len, heads * 128), jnp.bfloat16),
        grid_spec=pltpu.PrefetchScalarGridSpec(
            num_scalar_prefetch=1,
            grid=(heads // pair,),
            in_specs=[
                pl.BlockSpec((shards, kv, own), lambda g, _: (0, 0, 0)),
                pl.BlockSpec((pair, width, span_len), lambda g, _: (g, 0, 0)),
                pl.BlockSpec((lat, pair * 128), lambda g, _: (0, g)),
                pl.BlockSpec((lat, pair * 128), lambda g, _: (0, g)),
            ],
            out_specs=pl.BlockSpec((span_len, pair * 128), lambda g, _: (0, g)),
            scratch_shapes=[
                pltpu.VMEM((span_len // qb, (look + 1) * qb, qb), jnp.float32),
                pltpu.VMEM((pair, span_len, width), jnp.bfloat16),
                pltpu.VMEM((pair * 128, span_len), jnp.bfloat16),
                pltpu.VMEM((span_len, kv), jnp.bfloat16),
            ],
        ),
        compiler_params=pltpu.CompilerParams(
            dimension_semantics=("arbitrary",), vmem_limit_bytes=40 << 20
        ),
        cost_estimate=pl.CostEstimate(
            flops=12 * 10**9, bytes_accessed=20 << 20, transcendentals=8 << 20
        ),
    )(span_lengths, own_span, q_turned, key_weight, value_weight)


def decode_kernel(
    info_ref, q_ref, fresh_ref, spans_ref, cache_ref, out_ref, bufs, sems, m_ref, l_ref, acc_ref, *, lat, heads, blk, depth, scale
):
    owned = q_ref.shape[0]
    rows = q_ref.shape[1]

    def copy_of(r, t):
        slot = lax.rem(t, depth)
        place = info_ref[1, r] // blk * blk + t * blk
        place = pl.multiple_of(place, blk)

        @pl.when(info_ref[0, r] > 0)
        def _():
            own = spans_ref.shape[2]
            for c in range(blk // own):
                pltpu.make_async_copy(
                    spans_ref.at[place // own + c],
                    bufs.at[r, slot, :, c * own : (c + 1) * own],
                    sems.at[r, slot],
                ).start()

        @pl.when(info_ref[0, r] == 0)
        def _():
            pltpu.make_async_copy(
                cache_ref.at[r, :, pl.ds(place, blk)], bufs.at[r, slot], sems.at[r, slot]
            ).start()

    counts = []
    for r in range(owned):
        start, length = info_ref[1, r], info_ref[2, r]
        counts.append((start + length + blk - 1) // blk - start // blk)
    for r in range(owned):
        for t in range(depth - 1):
            pl.when(t < counts[r])(functools.partial(copy_of, r, jnp.int32(t)))
    for r in range(owned):
        start, length = info_ref[1, r], info_ref[2, r]
        base = start // blk * blk
        q = q_ref[r]
        fresh = fresh_ref[r]
        s = trans_dot(q, fresh)
        row_step = (lax.broadcasted_iota(jnp.int32, s.shape, 0) // heads) % 2
        col = lax.broadcasted_iota(jnp.int32, s.shape, 1)
        s = jnp.where(col <= row_step, s, NEGATIVE)
        m = jnp.max(s, axis=1, keepdims=True)
        w = jnp.exp2((s - m) * scale)
        l_ref[...] = jnp.broadcast_to(jnp.sum(w, axis=1, keepdims=True), l_ref.shape)
        m_ref[...] = jnp.broadcast_to(m, m_ref.shape)
        acc_ref[...] = jnp.dot(
            w.astype(jnp.bfloat16), fresh[:, :lat], preferred_element_type=jnp.float32
        )

        def step(t, carry):
            slot = lax.rem(t, depth)
            pl.when(t + depth - 1 < counts[r])(lambda: copy_of(r, t + depth - 1))
            pltpu.make_async_copy(
                cache_ref.at[r, :, pl.ds(0, blk)], bufs.at[r, slot], sems.at[r, slot]
            ).wait()
            keys = bufs[r, slot]
            s = jnp.dot(q, keys, preferred_element_type=jnp.float32)
            place = base + t * blk + lax.broadcasted_iota(jnp.int32, (1, blk), 1)
            hide = jnp.where((place >= start) & (place < start + length), 0.0, NEGATIVE)
            s = s + hide
            old = m_ref[:, :1]
            new = jnp.maximum(old, jnp.max(s, axis=1, keepdims=True))
            alpha = jnp.exp2((old - new) * scale)
            w = jnp.exp2((s - new) * scale)
            l_new = l_ref[:, :1] * alpha + jnp.sum(w, axis=1, keepdims=True)
            l_ref[...] = jnp.broadcast_to(l_new, l_ref.shape)
            m_ref[...] = jnp.broadcast_to(new, m_ref.shape)
            acc_ref[...] = acc_ref[...] * alpha + trans_dot(w.astype(jnp.bfloat16), keys[:lat])
            return carry

        lax.fori_loop(0, counts[r], step, 0)
        out_ref[r] = (acc_ref[...] / l_ref[:, :1]).astype(out_ref.dtype)


def decode_pallas(info, query, fresh, spans, cache, lat, heads, width, blk=512, depth=4):
    owned, rows, kv = query.shape
    return pl.pallas_call(
        functools.partial(
            decode_kernel,
            lat=lat,
            heads=heads,
            blk=blk,
            depth=depth,
            scale=math.log2(math.e) / math.sqrt(width),
        ),
        out_shape=jax.ShapeDtypeStruct((owned, rows, lat), jnp.bfloat16),
        in_specs=[
            pl.BlockSpec(memory_space=pltpu.SMEM),
            pl.BlockSpec(memory_space=pltpu.VMEM),
            pl.BlockSpec(memory_space=pltpu.VMEM),
            pl.BlockSpec(memory_space=pl.ANY),
            pl.BlockSpec(memory_space=pl.ANY),
        ],
        out_specs=pl.BlockSpec(memory_space=pltpu.VMEM),
        scratch_shapes=[
            pltpu.VMEM((owned, depth, kv, blk), jnp.bfloat16),
            pltpu.SemaphoreType.DMA((owned, depth)),
            pltpu.VMEM((rows, 128), jnp.float32),
            pltpu.VMEM((rows, 128), jnp.float32),
            pltpu.VMEM((rows, lat), jnp.float32),
        ],
        compiler_params=pltpu.CompilerParams(vmem_limit_bytes=40 << 20),
        cost_estimate=pl.CostEstimate(
            flops=5 * 10**9, bytes_accessed=10 << 20, transcendentals=2 << 20
        ),
    )(info, query, fresh, spans, cache)


def absorb_into(dq_ref, kw_ref, out_ref, flat, wide, heads, lat, step):
    rows = dq_ref.shape[0]
    flat[...] = dq_ref[:, :128].astype(jnp.float32)
    count = rows // heads
    for h in range(heads):
        mine = flat[pl.ds(h, count, stride=heads), :].astype(jnp.bfloat16)
        res = trans_dot(mine, kw_ref[:, h * 128 : (h + 1) * 128])
        for c in range(lat // 128):
            wide[c, pl.ds(h, count, stride=heads), :] = res[:, c * 128 : (c + 1) * 128]
    for c in range(lat // 128):
        out_ref[:, c * 128 : (c + 1) * 128] = wide[c].astype(jnp.bfloat16)
    out_ref[:, lat:] = dq_ref[:, 128:]


def absorb_kernel(dq_ref, kw_ref, out_ref, flat, wide, *, heads, lat):
    absorb_into(dq_ref, kw_ref, out_ref, flat, wide, heads, lat, 1)


def absorb_pallas(flat_queries, key_weight, heads):
    rows, width = flat_queries.shape
    lat = key_weight.shape[0]
    vm = pl.BlockSpec(memory_space=pltpu.VMEM)
    return pl.pallas_call(
        functools.partial(absorb_kernel, heads=heads, lat=lat),
        out_shape=jax.ShapeDtypeStruct((rows, lat + width - 128), jnp.bfloat16),
        in_specs=[vm, vm],
        out_specs=vm,
        scratch_shapes=[
            pltpu.VMEM((rows, 128), jnp.float32),
            pltpu.VMEM((lat // 128, rows, 128), jnp.float32),
        ],
        compiler_params=pltpu.CompilerParams(vmem_limit_bytes=24 << 20),
    )(flat_queries, key_weight)


def project_into(x_ref, vw_ref, out_ref, wide, heads, lat):
    rows = x_ref.shape[0]
    count = rows // heads
    for c in range(lat // 128):
        wide[c] = x_ref[:, c * 128 : (c + 1) * 128].astype(jnp.float32)
    for h in range(heads):
        mine = jnp.concatenate(
            [wide[c, pl.ds(h, count, stride=heads), :] for c in range(lat // 128)], axis=1
        ).astype(jnp.bfloat16)
        out_ref[:, h * 128 : (h + 1) * 128] = jnp.dot(
            mine, vw_ref[:, h * 128 : (h + 1) * 128], preferred_element_type=jnp.float32
        ).astype(jnp.bfloat16)


def project_kernel(x_ref, vw_ref, out_ref, wide, *, heads, lat):
    project_into(x_ref, vw_ref, out_ref, wide, heads, lat)


def project_pallas(flat_latent, value_weight, heads):
    rows, lat = flat_latent.shape
    vm = pl.BlockSpec(memory_space=pltpu.VMEM)
    return pl.pallas_call(
        functools.partial(project_kernel, heads=heads, lat=lat),
        out_shape=jax.ShapeDtypeStruct((rows // heads, heads * 128), jnp.bfloat16),
        in_specs=[vm, vm],
        out_specs=vm,
        scratch_shapes=[pltpu.VMEM((lat // 128, rows, 128), jnp.float32)],
        compiler_params=pltpu.CompilerParams(vmem_limit_bytes=24 << 20),
    )(flat_latent, value_weight)


def on_device(
    latent_rows,
    pre_queries,
    pre_lengths,
    owner_map,
    context_cache,
    context_lengths,
    new_latent,
    dec_queries,
    key_weight,
    value_weight,
):
    steps, rows_local, heads, width = dec_queries.shape
    if heads % 16 or latent_rows.shape[0] % 128:
        return plain_on_device(
            latent_rows,
            pre_queries,
            pre_lengths,
            owner_map,
            context_cache,
            context_lengths,
            new_latent,
            dec_queries,
            key_weight,
            value_weight,
        )
    head_rank = lax.axis_index("head")
    batch_rank = lax.axis_index("batch")
    ranks = lax.axis_size("head")
    span_len = pre_queries.shape[0]
    kv = latent_rows.shape[1]
    lat = key_weight.shape[0]
    owned = context_cache.shape[0]
    span_lengths = lax.dynamic_index_in_dim(pre_lengths, batch_rank, 0, keepdims=False)
    flat_owner, flat_start, flat_length = request_table(pre_lengths, owner_map, span_len)
    row_ids = batch_rank * rows_local + head_rank * owned + jnp.arange(owned, dtype=jnp.int32)
    matches = (flat_owner[None, :] == row_ids[:, None]).astype(jnp.int32)
    is_target = jnp.sum(matches, axis=1)
    first_row = jnp.sum(matches * flat_start[None, :], axis=1)
    prompt_len = jnp.sum(matches * flat_length[None, :], axis=1)
    first_row = lax.rem(first_row + batch_rank * span_len, 2 * span_len) * is_target
    effective = jnp.where(is_target > 0, prompt_len, context_lengths)
    info = jnp.stack([is_target, first_row, effective])
    fresh = jnp.pad(
        jnp.transpose(new_latent, (1, 0, 2)), ((0, 0), (0, 128 - steps), (0, 0))
    )
    absorbed = absorb_pallas(dec_queries.reshape(-1, width), key_weight, heads)
    query_all = absorbed.reshape(steps, rows_local, heads, kv)
    turned = jnp.transpose(latent_rows)
    half = kv // 2
    upper = lax.all_gather(turned[:half], "head", axis=0)
    turned, upper = lax.optimization_barrier((turned, upper))
    lower = lax.all_gather(turned[half:], "head", axis=0)
    own_span = jnp.concatenate([upper, lower], axis=1)
    other_span = from_partner(own_span, "batch", 0)
    all_spans = jnp.concatenate([own_span, other_span], axis=0)
    got = lax.all_to_all(query_all, "head", split_axis=1, concat_axis=2, tiled=True)
    query = jnp.transpose(got, (1, 0, 2, 3)).reshape(owned, steps * ranks * heads, kv)
    latent_out = decode_pallas(
        info, query, fresh, all_spans, jnp.transpose(context_cache, (0, 2, 1)), lat, ranks * heads, width
    )
    back = jnp.transpose(latent_out.reshape(owned, steps, ranks * heads, lat), (1, 0, 2, 3))
    returned = lax.all_to_all(back, "head", split_axis=2, concat_axis=1, tiled=True)
    prefill_out = prefill_pallas(own_span, pre_queries, span_lengths, key_weight, value_weight)
    decode_out = project_pallas(returned.reshape(-1, lat), value_weight, heads)
    return (prefill_out, decode_out.reshape(steps, rows_local, heads * 128))


def solution(mesh):
    placed = (
        P(("groups", "batch", "head"), None),
        P(("groups", "batch"), "head", None),
        P("groups", None),
        P("groups", None),
        P(("groups", "batch", "head"), None, None),
        P(("groups", "batch", "head")),
        P("groups", ("batch", "head"), None),
        P("groups", "batch", "head", None),
        P(None, "head"),
        P(None, "head"),
    )
    return jax.shard_map(
        on_device,
        mesh=mesh,
        in_specs=placed,
        out_specs=(P(("groups", "batch"), "head"), P("groups", "batch", "head")),
        check_vma=False,
    )
```

profile of v0, /device:TPU:0, one launch (start us, length us, event | category | flops | bytes accessed | tf_op | source)
XLA Modules:
  0.0 163.5 jit_solution(17169609848474895392)
XLA Ops:
  0.6 0.0 copy-start.4
  0.6 0.0 copy-start
  0.6 1.0 slice.8
  1.7 33.2 %all-gather = bf16[2304,128]{1,0:T(8,128)(2,1)S(1)} all-gather(bf16[288,128]{1,0:T(8,128)(2,1)S(1)} %slice.8), channel_id=2, replica_groups=mesh['groups'=2,'head'=8,'batch'=2] {'head'}, dimensions={0}, use_global_device_ids=true | all-gather | bytes 663552 | tf_op jit(solution)/shard_map/all_gather | solution.py:530
  34.9 0.0 copy-start.7
  34.9 0.9 slice.7
  35.9 31.4 %all-gather.1 = bf16[2304,128]{1,0:T(8,128)(2,1)S(1)} all-gather(bf16[288,128]{1,0:T(8,128)(2,1)S(1)} %slice.7), channel_id=3, replica_groups=mesh['groups'=2,'head'=8,'batch'=2] {'head'}, dimensions={0}, use_global_device_ids=true | all-gather | bytes 663552 | tf_op jit(solution)/shard_map/all_gather | solution.py:532
  67.3 0.0 copy-start.8
  67.3 0.1 pad_maximum_fusion.1.shards_ref
  67.3 0.1 collective-permute-start
  67.4 0.0 copy-done.7
  67.4 0.6 copy-done.8
  68.1 0.0 copy-done.4
  68.1 0.0 copy-done
  68.1 0.0 copy-start.9
  68.1 0.0 copy-start.11
  68.1 1.1 shard_map.114
  69.2 0.9 copy.24
  70.1 5.8 %all-to-all-start = ((bf16[2,16,16,576]{3,2,0,1:T(8,128)(2,1)}), bf16[2,16,16,576]{3,2,0,1:T(8,128)(2,1)}, u32[]{:S(2)}, u32[]{:S(2)}) async-start(bf16[2,16,16,576]{3,2,0,1:T(8,128)(2,1)} %copy.24), calls=%async_computation | async-start | bytes 1310720 | tf_op jit(solution)/shard_map/all_to_all | solution.py:536
  75.9 0.0 copy-done.10
  75.9 0.1 mul.55
  76.0 0.2 reduce_window_sum.11
  76.1 0.1 subtract_add_fusion
  76.2 0.1 mul.50
  76.3 0.0 copy-done.12
  76.3 0.1 eq.15
  76.4 0.0 copy-done.9
  76.4 0.8 pad.4.fresh_ref
  77.2 0.2 fusion.1
  77.4 0.0 copy-done.11
  77.4 15.9 %all-to-all-done = bf16[2,16,16,576]{3,2,0,1:T(8,128)(2,1)} async-done(((bf16[2,16,16,576]{3,2,0,1:T(8,128)(2,1)}), bf16[2,16,16,576]{3,2,0,1:T(8,128)(2,1)}, u32[]{:S(2)}, u32[]{:S(2)}) %all-to-all-start) | async-done | bytes 589856 | tf_op jit(solution)/shard_map/all_to_all | solution.py:536
  93.3 1.1 copy.25
  94.5 0.0 copy-start.3
  94.5 0.0 collective-permute-done
  94.5 1.8 %pad_maximum_fusion.spans_ref = bf16[16,576,128]{2,1,0:T(8,128)(2,1)S(1)} fusion(bf16[8,576,128]{2,1,0:T(8,128)(2,1)} %collective-permute-done, bf16[8,288,128]{2,1,0:T(8,128)(2,1)} %bitcast.45, bf16[8,288,128]{2,1,0:T(8,128)(2,1)} %bitcast.43), kind=kLoop, calls=%fused_computation | loop fusion | flops 7077888 | bytes 4718592 | tf_op jit(solution)/shard_map/concatenate | solution.py:535
  96.3 0.0 copy-done.3
  96.3 0.0 copy-start.5
  96.3 3.7 %copy-done.5 = bf16[2,4096,576]{1,2,0:T(8,128)(2,1)S(1)} copy-done((bf16[2,4096,576]{1,2,0:T(8,128)(2,1)S(1)}, bf16[2,4096,576]{1,2,0:T(8,128)(2,1)}, u32[]{:S(2)}) %copy-start.5) | copy-done | bytes 9437208
  100.0 3.9 %shard_map.115 = bf16[2,256,512]{2,1,0:T(8,128)(2,1)S(1)} custom-call(s32[3,2]{1,0:T(4,128)S(1)} %pad_add_fusion.info_ref, bf16[2,256,576]{2,1,0:T(8,128)(2,1)S(1)} %bitcast.37, bf16[2,128,576]{2,1,0:T(8,128)(2,1)S(1)} %copy-done.3, bf16[16,576,128]{2,1,0:T(8,128)(2,1)S(1)} %pad_maximum_fusion.spans_ref, bf16[2,576,4096]{2,1,0:T(8,128)(2,1)S(1)} %bitcast.40), custom_call_target="tpu_custom_call" | custom-call | flops 5000000000 | bytes 10485760 | tf_op jit(solution)/shard_map/pallas_call | solution.py:382
  104.0 1.3 copy.32
  105.3 10.0 %all-to-all-start.1 = ((bf16[2,2,128,512]{3,1,0,2:T(2,128)(2,1)}), bf16[2,2,128,512]{3,1,0,2:T(2,128)(2,1)}, u32[]{:S(2)}, u32[]{:S(2)}) async-start(bf16[2,2,128,512]{3,1,0,2:T(2,128)(2,1)} %bitcast.46), calls=%async_computation.1 | async-start | bytes 1048576 | tf_op jit(solution)/shard_map/all_to_all | solution.py:542
  115.3 1.6 copy-done.1
  116.9 2.8 %copy-done.6 = bf16[1024,16,192]{0,2,1:T(8,128)(2,1)S(1)} copy-done((bf16[1024,16,192]{0,2,1:T(8,128)(2,1)S(1)}, bf16[1024,16,192]{0,2,1:T(8,128)(2,1)}, u32[]{:S(2)}) %copy-start.6) | copy-done | bytes 6291480
  119.7 40.5 %shard_map.113 = bf16[1024,2048]{1,0:T(8,128)(2,1)} custom-call(s32[4]{0:T(128)S(1)} %dynamic-slice_bitcast_fusion.lens_ref, bf16[8,576,128]{2,1,0:T(8,128)(2,1)S(1)} %pad_maximum_fusion.1.shards_ref, bf16[16,192,1024]{2,1,0:T(8,128)(2,1)S(1)} %bitcast.41, bf16[512,2048]{1,0:T(8,128)(2,1)S(1)} %copy-done, bf16[512,2048]{1,0:T(8,128)(2,1)S(1)} %copy-done.1), custom_call_target="tpu_custom_call" | custom-call | flops 12000000000 | bytes 20971520 | tf_op jit(solution)/shard_map/pallas_call | solution.py:275
  160.2 0.0 all-to-all-done.1
  160.2 1.3 copy.28
  161.5 0.4 copy-done.2
  161.9 1.5 shard_map.116
  (13 shorter events, 0.1 us)
Async XLA Ops:
  0.6 67.4 %copy-start.4 = (bf16[2,16,16,192]{3,2,1,0:T(8,128)(2,1)S(1)}, bf16[2,16,16,192]{3,2,1,0:T(8,128)(2,1)}, u32[]{:S(2)}) copy-start(bf16[2,16,16,192]{3,2,1,0:T(8,128)(2,1)} %param.17) | copy-start | bytes 589828
  0.6 67.4 %copy-start = (bf16[512,2048]{1,0:T(8,128)(2,1)S(1)}, bf16[512,2048]{1,0:T(8,128)(2,1)}, u32[]{:S(2)}) copy-start(bf16[512,2048]{1,0:T(8,128)(2,1)} %kw_ref.3) | copy-start | bytes 6291460
  34.9 32.5 %copy-start.7 = (bf16[2304,128]{1,0:T(8,128)(2,1)}, bf16[2304,128]{1,0:T(8,128)(2,1)S(1)}, u32[]{:S(2)}) copy-start(bf16[2304,128]{1,0:T(8,128)(2,1)S(1)} %all-gather) | copy-start | bytes 1769476
  67.3 0.8 copy-start.8
  67.3 27.1 %collective-permute-start = (bf16[8,576,128]{2,1,0:T(8,128)(2,1)S(1)}, bf16[8,576,128]{2,1,0:T(8,128)(2,1)}, u32[]{:S(2)}, u32[]{:S(2)}) collective-permute-start(bf16[8,576,128]{2,1,0:T(8,128)(2,1)S(1)} %pad_maximum_fusion.1.shards_ref), channel_id=1, source_target_pairs={{0,1},{1,0},{2,3},{3,2},{4,5},{5,4},{6,7},{7,6},{8,9},{9,8},{10,11... | collective-permute-start | bytes 3538952 | tf_op jit(solution)/shard_map/ppermute | solution.py:20
  68.1 7.8 %copy-start.10 = (s32[2,4]{1,0:T(2,128)S(1)}, s32[2,4]{1,0:T(2,128)}, u32[]{:S(2)}) copy-start(s32[2,4]{1,0:T(2,128)} %param.12) | copy-start | bytes 100
  68.1 8.2 %copy-start.12 = (s32[2,4]{1,0:T(2,128)S(1)}, s32[2,4]{1,0:T(2,128)}, u32[]{:S(2)}) copy-start(s32[2,4]{1,0:T(2,128)} %param.13) | copy-start | bytes 100
  68.1 8.3 %copy-start.9 = (bf16[2,2,576]{2,1,0:T(2,128)(2,1)S(1)}, bf16[2,2,576]{2,1,0:T(2,128)(2,1)}, u32[]{:S(2)}) copy-start(bf16[2,2,576]{2,1,0:T(2,128)(2,1)} %param.16) | copy-start | bytes 13828
  68.1 9.3 %copy-start.11 = (s32[2]{0:T(128)S(1)}, s32[2]{0:T(128)}, u32[]{:S(2)}) copy-start(s32[2]{0:T(128)} %param.15) | copy-start | bytes 28
  70.1 23.2 %all-to-all-start = ((bf16[2,16,16,576]{3,2,0,1:T(8,128)(2,1)}), bf16[2,16,16,576]{3,2,0,1:T(8,128)(2,1)}, u32[]{:S(2)}, u32[]{:S(2)}) async-start(bf16[2,16,16,576]{3,2,0,1:T(8,128)(2,1)} %copy.24), calls=%async_computation | async-start | bytes 1310720 | tf_op jit(solution)/shard_map/all_to_all | solution.py:536
  94.5 1.9 %copy-start.3 = (bf16[2,128,576]{2,1,0:T(8,128)(2,1)S(1)}, bf16[2,128,576]{2,1,0:T(8,128)(2,1)}, u32[]{:S(2)}) copy-start(bf16[2,128,576]{2,1,0:T(8,128)(2,1)} %pad.4.fresh_ref) | copy-start | bytes 884740
  96.3 3.7 %copy-start.5 = (bf16[2,4096,576]{1,2,0:T(8,128)(2,1)S(1)}, bf16[2,4096,576]{1,2,0:T(8,128)(2,1)}, u32[]{:S(2)}) copy-start(bf16[2,4096,576]{1,2,0:T(8,128)(2,1)} %param.14) | copy-start | bytes 28311556
  105.3 54.9 %all-to-all-start.1 = ((bf16[2,2,128,512]{3,1,0,2:T(2,128)(2,1)}), bf16[2,2,128,512]{3,1,0,2:T(2,128)(2,1)}, u32[]{:S(2)}, u32[]{:S(2)}) async-start(bf16[2,2,128,512]{3,1,0,2:T(2,128)(2,1)} %bitcast.46), calls=%async_computation.1 | async-start | bytes 1048576 | tf_op jit(solution)/shard_map/all_to_all | solution.py:542
  115.3 1.6 copy-start.1
  116.9 2.8 %copy-start.6 = (bf16[1024,16,192]{0,2,1:T(8,128)(2,1)S(1)}, bf16[1024,16,192]{0,2,1:T(8,128)(2,1)}, u32[]{:S(2)}) copy-start(bf16[1024,16,192]{0,2,1:T(8,128)(2,1)} %param.11) | copy-start | bytes 18874372
  160.2 1.7 %copy-start.2 = (bf16[512,2048]{1,0:T(8,128)(2,1)S(1)}, bf16[512,2048]{1,0:T(8,128)(2,1)}, u32[]{:S(2)}) copy-start(bf16[512,2048]{1,0:T(8,128)(2,1)} %vw_ref.3) | copy-start | bytes 6291460
where the time goes:
time: 166 us; the launch traced here: 163 us
  blocking collectives  64.6 us (39%)
  Pallas kernels  47.1 us (28%)
  local copies, waits for them, and re-layouts  16.8 us (10%)
  waiting for transfers between devices  15.9 us (10%)
  starting transfers between devices  15.8 us (10%)
  other arithmetic  2.41 us (1%)
    pallas_call x1, Pallas kernels, prefill_pallas(): pl.pallas_call(functools.partial(prefill_kernel, lat=lat, qb=qb, look=loo...  40.5 us
    all_gather x1, blocking collectives, on_device(): upper = lax.all_gather(turned[:half], 'head', axis=0)  33.2 us
    all_gather x1, blocking collectives, on_device(): lower = lax.all_gather(turned[half:], 'head', axis=0)  31.4 us
    all_to_all x1, waiting for transfers between devices, on_device(): lax.all_to_all(query_all, 'head', split_axis=1, concat_axis=2, tiled=True)  15.9 us
    all_to_all x1, starting transfers between devices, on_device(): lax.all_to_all(back, 'head', split_axis=2, concat_axis=1, tiled=True)  10 us
    unnamed x27, local copies, waits for them, and re-layouts  9.14 us
    all_to_all x1, starting transfers between devices, on_device(): lax.all_to_all(query_all, 'head', split_axis=1, concat_axis=2, tiled=True)  5.76 us
    pallas_call x1, Pallas kernels, decode_pallas(): pl.pallas_call(functools.partial(decode_kernel, lat=lat, heads=heads, blk...  3.94 us
  transfers between devices with their start and end apart: 3, of which 1 were waited for; matrix products, arithmetic and copies ran while one was open for 2% of the time, Pallas kernels for 25%

commit v1 on v0

v1 whole, which is shorter than its diff:
```python
import functools
import math

import jax
import jax.numpy as jnp
from jax import lax
from jax.experimental import pallas as pl
from jax.experimental.pallas import tpu as pltpu
from jax.sharding import PartitionSpec as P

BLK = 512


NEGATIVE = -1e30


def from_partner(value, axis, distance):
    mask = 2**distance
    pairs = [(source, source ^ mask) for source in range(lax.axis_size(axis))]
    return lax.ppermute(value, axis, pairs)


def request_table(pre_lengths, owner_map, span_len):
    seg_ends = jnp.cumsum(pre_lengths, axis=1)
    span_base = jnp.arange(pre_lengths.shape[0], dtype=jnp.int32)[:, None] * span_len
    seg_starts = seg_ends - pre_lengths + span_base
    return (owner_map.reshape(-1), seg_starts.reshape(-1), pre_lengths.reshape(-1))


def prefill_heads(own_span, queries, span_lengths, key_weight, value_weight):
    span_len, head_count, query_width = queries.shape
    head_size = key_weight.shape[1] // head_count
    lat_width = key_weight.shape[0]
    score_scale = 1.0 / math.sqrt(query_width)
    latent = own_span[:, :lat_width]
    rope_keys = own_span[:, lat_width:]
    keys_nope = (
        jnp.dot(latent, key_weight, preferred_element_type=jnp.float32)
        .astype(jnp.bfloat16)
        .reshape(span_len, head_count, head_size)
    )
    values = (
        jnp.dot(latent, value_weight, preferred_element_type=jnp.float32)
        .astype(jnp.bfloat16)
        .reshape(span_len, head_count, head_size)
    )
    scores = jnp.einsum(
        "qhd,khd->hqk", queries[:, :, :head_size], keys_nope, preferred_element_type=jnp.float32
    )
    scores = scores + jnp.einsum(
        "qhr,kr->hqk", queries[:, :, head_size:], rope_keys, preferred_element_type=jnp.float32
    )
    scores = scores * score_scale
    seg_ends = jnp.cumsum(span_lengths)
    places = jnp.arange(span_len, dtype=jnp.int32)
    segment = jnp.sum((places[:, None] >= seg_ends[None, :]).astype(jnp.int32), axis=1)
    allowed = (segment[:, None] == segment[None, :]) & (places[None, :] <= places[:, None])
    masked = jnp.where(allowed[None], scores, NEGATIVE)
    peak_score = jnp.max(masked, axis=2, keepdims=True)
    weights = jnp.exp(masked - peak_score)
    weight_sum = jnp.sum(weights, axis=2)
    mixed_out = jnp.einsum(
        "hqk,khd->qhd", weights.astype(jnp.bfloat16), values, preferred_element_type=jnp.float32
    )
    mixed_out = mixed_out / jnp.transpose(weight_sum)[:, :, None]
    return mixed_out.astype(jnp.bfloat16).reshape(span_len, head_count * head_size)


def plain_on_device(
    latent_rows,
    pre_queries,
    pre_lengths,
    owner_map,
    context_cache,
    context_lengths,
    new_latent,
    dec_queries,
    key_weight,
    value_weight,
):
    head_rank = lax.axis_index("head")
    batch_rank = lax.axis_index("batch")
    span_len = pre_queries.shape[0]
    kv_width = latent_rows.shape[1]
    own_span = lax.all_gather(latent_rows, "head", axis=0, tiled=True)
    other_span = from_partner(own_span, "batch", 0)
    first_span = jnp.where(batch_rank == 0, own_span, other_span)
    second_span = jnp.where(batch_rank == 0, other_span, own_span)
    all_spans = jnp.concatenate([first_span, second_span], axis=0)
    span_lengths = lax.dynamic_index_in_dim(pre_lengths, batch_rank, 0, keepdims=False)
    prefill_out = prefill_heads(own_span, pre_queries, span_lengths, key_weight, value_weight)
    step_total, rows_local, head_count, query_width = dec_queries.shape
    lat_width = key_weight.shape[0]
    head_size = key_weight.shape[1] // head_count
    owned_rows = context_cache.shape[0]
    score_scale = 1.0 / math.sqrt(query_width)
    key_heads = key_weight.reshape(lat_width, head_count, head_size)
    value_heads = value_weight.reshape(lat_width, head_count, head_size)
    absorbed = jnp.einsum(
        "srhd,lhd->srhl",
        dec_queries[..., :head_size],
        key_heads,
        preferred_element_type=jnp.float32,
    ).astype(jnp.bfloat16)
    query_all = jnp.concatenate([absorbed, dec_queries[..., head_size:]], axis=3)
    flat_owner, flat_start, flat_length = request_table(pre_lengths, owner_map, span_len)
    row_ids = (
        batch_rank * rows_local + head_rank * owned_rows + jnp.arange(owned_rows, dtype=jnp.int32)
    )
    matches = (flat_owner[None, :] == row_ids[:, None]).astype(jnp.int32)
    is_target = jnp.sum(matches, axis=1) > 0
    first_row = jnp.sum(matches * flat_start[None, :], axis=1)
    prompt_len = jnp.sum(matches * flat_length[None, :], axis=1)
    effective = jnp.where(is_target, prompt_len, context_lengths)
    padded = jnp.concatenate([all_spans, jnp.zeros((span_len, kv_width), all_spans.dtype)], axis=0)
    replaced = jax.vmap(lambda offset: lax.dynamic_slice_in_dim(padded, offset, span_len, 0))(
        first_row
    )
    front_rows = jnp.where(is_target[:, None, None], replaced, context_cache[:, :span_len])
    front_blocks = span_len // BLK
    needed = (jnp.max(effective) + BLK - 1) // BLK
    fresh_latent = new_latent[..., :lat_width]
    owned_query = lax.all_to_all(query_all, "head", split_axis=1, concat_axis=2, tiled=True)
    fresh_scores = (
        jnp.einsum("srhk,jrk->srhj", owned_query, new_latent, preferred_element_type=jnp.float32)
        * score_scale
    )
    visible = (
        jnp.arange(new_latent.shape[0], dtype=jnp.int32)[None, :]
        <= jnp.arange(step_total, dtype=jnp.int32)[:, None]
    )
    fresh_scores = jnp.where(visible[:, None, None, :], fresh_scores, NEGATIVE)
    peak_score = jnp.max(fresh_scores, axis=3)
    weights = jnp.exp(fresh_scores - peak_score[..., None])
    weight_sum = jnp.sum(weights, axis=3)
    running = jnp.einsum(
        "srhj,jrl->srhl",
        weights.astype(jnp.bfloat16),
        fresh_latent,
        preferred_element_type=jnp.float32,
    )

    def advance(block_index, state_tuple, source):
        old_peak, old_sum, old_running = state_tuple
        key_block = lax.dynamic_slice_in_dim(source, block_index * BLK, BLK, 1)
        scores = (
            jnp.einsum("srhk,rtk->srht", owned_query, key_block, preferred_element_type=jnp.float32)
            * score_scale
        )
        places = block_index * BLK + jnp.arange(BLK, dtype=jnp.int32)
        in_context = places[None, :] < effective[:, None]
        scores = jnp.where(in_context[None, :, None, :], scores, NEGATIVE)
        new_peak = jnp.maximum(old_peak, jnp.max(scores, axis=3))
        factor = jnp.exp(old_peak - new_peak)
        block_weights = jnp.exp(scores - new_peak[..., None])
        new_sum = old_sum * factor + jnp.sum(block_weights, axis=3)
        new_running = old_running * factor[..., None] + jnp.einsum(
            "srht,rtl->srhl",
            block_weights.astype(jnp.bfloat16),
            key_block[..., :lat_width],
            preferred_element_type=jnp.float32,
        )
        return (new_peak, new_sum, new_running)

    state_tuple = lax.fori_loop(
        0,
        jnp.minimum(needed, front_blocks),
        lambda block_index, state_now: advance(block_index, state_now, front_rows),
        (peak_score, weight_sum, running),
    )
    state_tuple = lax.fori_loop(
        front_blocks,
        jnp.maximum(needed, front_blocks),
        lambda block_index, state_now: advance(block_index, state_now, context_cache),
        state_tuple,
    )
    latent_out = (state_tuple[2] / state_tuple[1][..., None]).astype(jnp.bfloat16)
    returned = lax.all_to_all(latent_out, "head", split_axis=2, concat_axis=1, tiled=True)
    projected = jnp.einsum(
        "srhl,lhd->srhd", returned, value_heads, preferred_element_type=jnp.float32
    ).astype(jnp.bfloat16)
    decode_out = projected.reshape(query_all.shape[0], rows_local, head_count * head_size)
    return (prefill_out, decode_out)


def trans_dot(left, right):
    return lax.dot_general(
        left, right, (((1,), (1,)), ((), ())), preferred_element_type=jnp.float32
    )


MESH = pl.DeviceIdType.MESH


def place_of(rank, ranks):
    odd = rank % 2
    return (1 - odd) * (rank // 2) + odd * (ranks - 1 - rank // 2)


def rank_at(place, ranks):
    late = place // (ranks // 2)
    return (1 - late) * (2 * place) + late * (2 * (ranks - 1 - place) + 1)


def start_marks(ends, keys, vals, hot, tri, rows_ref, lat):
    pair, span_len, _ = keys.shape
    segs = len(ends)
    marks = keys.shape[2] - 128 - (rows_ref.shape[1] - lat)
    where = lax.broadcasted_iota(jnp.int32, (span_len, marks), 0)
    lane = lax.broadcasted_iota(jnp.int32, (span_len, marks), 1)
    place = lax.broadcasted_iota(jnp.int32, (marks, span_len), 1)
    line = lax.broadcasted_iota(jnp.int32, (marks, span_len), 0)
    mine = jnp.zeros((span_len, marks), jnp.int32)
    seen = jnp.zeros((marks, span_len), jnp.int32)
    for k in range(segs - 1):
        mine = mine + (where >= ends[k]).astype(jnp.int32)
        seen = seen + (place >= ends[k]).astype(jnp.int32)
    mark = jnp.where((lane < segs) & (lane != mine), NEGATIVE, 0.0).astype(jnp.bfloat16)
    hot[...] = jnp.where(line == seen, 1.0, 0.0).astype(jnp.bfloat16)
    for p in range(pair):
        keys[p, :, 128 : keys.shape[2] - marks] = rows_ref[:, lat:]
        keys[p, :, keys.shape[2] - marks :] = mark
        vals[p, 128:, :] = jnp.ones((vals.shape[1] - 128, span_len), jnp.bfloat16)
    size = tri.shape[0]
    key_at = lax.broadcasted_iota(jnp.int32, (size, size), 0)
    query_at = lax.broadcasted_iota(jnp.int32, (size, size), 1)
    tri[...] = jnp.where(key_at <= query_at, 0.0, NEGATIVE)


def attend_pair(g, kw, vw, qs, spans_ref, rows_ref, keys, vals, hot, tri, part_ref, lat, look, scale):
    pair, span_len, _ = keys.shape
    qb = tri.shape[0]
    wide = pair * 128
    columns = pl.ds(pl.multiple_of(g * wide, wide), wide)
    made = jnp.dot(rows_ref[:, :lat], kw[:, columns], preferred_element_type=jnp.float32)
    made = made.astype(jnp.bfloat16)
    for p in range(pair):
        keys[p, :, :128] = made[:, p * 128 : (p + 1) * 128]
    turned = jnp.transpose(vw[:, columns])
    for c in range(span_len // 256):
        latents = jnp.concatenate(
            [spans_ref[2 * c, :lat, :], spans_ref[2 * c + 1, :lat, :]], axis=1
        )
        value = jnp.dot(turned, latents, preferred_element_type=jnp.float32).astype(jnp.bfloat16)
        for p in range(pair):
            vals[p, :128, c * 256 : (c + 1) * 256] = value[p * 128 : (p + 1) * 128]
    for i in range(span_len // qb):
        lo, hi = max(i - look, 0) * qb, (i + 1) * qb
        for p in range(pair):
            query = jnp.concatenate(
                [qs[g * pair + p, :, i * qb : hi], hot[:, i * qb : hi]], axis=0
            )
            s = jnp.dot(keys[p, lo:hi, :], query, preferred_element_type=jnp.float32)
            last = s[hi - lo - qb :] + tri[...]
            s = last if hi - lo == qb else jnp.concatenate([s[: hi - lo - qb], last], axis=0)
            m = jnp.max(s, axis=0, keepdims=True)
            w = jnp.exp2((s - m) * scale).astype(jnp.bfloat16)
            o = jnp.dot(vals[p, :, lo:hi], w, preferred_element_type=jnp.float32)
            o = o[:128] * (1.0 / o[128:129])
            part_ref[i * qb : hi, pl.ds(pl.multiple_of(g * wide + p * 128, 128), 128)] = (
                jnp.transpose(o.astype(jnp.bfloat16))
            )


def absorb_into(dq, kw, sent, flat, wide, heads, lat):
    rows = dq.shape[0]
    ranks, owned, block, _ = sent.shape
    steps = block // heads
    local = ranks * owned
    flat[...] = dq[:, :128].astype(jnp.float32)
    for h in range(heads):
        mine = flat[pl.ds(h, rows // heads, stride=heads), :].astype(jnp.bfloat16)
        res = trans_dot(mine, kw[:, h * 128 : (h + 1) * 128])
        for s in range(steps):
            for c in range(lat // 128):
                wide[c, pl.ds(s * heads + h, local, stride=block), :] = res[
                    s * local : (s + 1) * local, c * 128 : (c + 1) * 128
                ]
    for p in range(ranks):
        for r in range(owned):
            at = p * owned + r
            for c in range(lat // 128):
                sent[p, r, :, c * 128 : (c + 1) * 128] = wide[
                    c, at * block : (at + 1) * block
                ].astype(jnp.bfloat16)
            for s in range(steps):
                start = (s * local + at) * heads
                sent[p, r, s * heads : (s + 1) * heads, lat:] = dq[start : start + heads, 128:]


def span_ends(lens_ref, batch_rank):
    ends = []
    total = 0
    for k in range(lens_ref.shape[1]):
        total = total + lens_ref[batch_rank, k]
        ends.append(total)
    return ends


def gather_kernel(
    lens_ref, shard_hbm, dq_hbm, kw_hbm, vw_hbm, q_hbm,
    spans_ref, rows_ref, got_ref, part_ref,
    kw, vw, qs, dq, flat, wide, sent, keys, vals, hot, tri,
    load_sems, ring_send, ring_recv, swap_sems, give_sems, take_sems,
    *, lat, ranks, heads, look, scale
):
    me = lax.axis_index("head")
    batch_rank = lax.axis_index("batch")
    place = place_of(me, ranks)
    right = rank_at((place + 1) % ranks, ranks)
    left = rank_at((place + ranks - 1) % ranks, ranks)
    some = qs.shape[0]
    loads = [
        pltpu.make_async_copy(dq_hbm, dq, load_sems.at[0]),
        pltpu.make_async_copy(kw_hbm, kw, load_sems.at[1]),
        pltpu.make_async_copy(shard_hbm, spans_ref.at[me], load_sems.at[2]),
        pltpu.make_async_copy(vw_hbm.at[:, : some * 128], vw, load_sems.at[3]),
        pltpu.make_async_copy(q_hbm.at[:some], qs, load_sems.at[4]),
    ]
    barrier = pltpu.get_barrier_semaphore()
    for k in range(1, ranks):
        pl.semaphore_signal(
            barrier, inc=1, device_id={"head": (me + k) % ranks}, device_id_type=MESH
        )
    pl.semaphore_signal(
        barrier, inc=1, device_id={"batch": 1 - batch_rank}, device_id_type=MESH
    )
    for load in loads:
        load.start()
    pl.semaphore_wait(barrier, ranks)

    half = shard_hbm.shape[0] // 2
    most = ranks // 2

    def hop(way, part, t):
        back = t - 1 if way == 0 else ranks - t + 1
        origin = rank_at((place + ranks - back) % ranks, ranks)
        rows = pl.ds(part * half, half)
        source = shard_hbm.at[rows] if t == 1 else spans_ref.at[origin, rows]
        return pltpu.make_async_remote_copy(
            src_ref=source,
            dst_ref=spans_ref.at[origin, rows],
            send_sem=ring_send.at[way, part, t - 1],
            recv_sem=ring_recv.at[way, part, t - 1],
            device_id={"head": right if way == 0 else left},
            device_id_type=MESH,
        )

    def hops(way, part):
        return most if way == part else most - 1

    streams = [(0, 0), (1, 1), (0, 1), (1, 0)]
    for way, part in streams:
        hop(way, part, 1).start()
    loads[0].wait()
    loads[1].wait()
    absorb_into(dq, kw, sent, flat, wide, heads, lat)

    own = shard_hbm.shape[1]

    def turn(origin):
        rows_ref[pl.ds(pl.multiple_of(origin * own, own), own), :] = jnp.transpose(
            spans_ref[origin]
        )

    loads[2].wait()
    turn(me)
    for t in range(1, most + 1):
        for way, part in streams:
            if t <= hops(way, part):
                hop(way, part, t).wait_recv()
                if t < hops(way, part):
                    hop(way, part, t + 1).start()
        turn(rank_at((place + ranks - t) % ranks, ranks))
        if t < most:
            turn(rank_at((place + t) % ranks, ranks))

    gives = []
    for k in range(1, ranks):
        peer = (me + k) % ranks
        gives.append(
            pltpu.make_async_remote_copy(
                src_ref=sent.at[peer],
                dst_ref=got_ref.at[me],
                send_sem=give_sems.at[k - 1],
                recv_sem=take_sems.at[k - 1],
                device_id={"head": peer},
                device_id_type=MESH,
            )
        )
    for give in gives:
        give.start()
    keep = pltpu.make_async_copy(sent.at[me], got_ref.at[me], load_sems.at[5])
    keep.start()
    swap = pltpu.make_async_remote_copy(
        src_ref=spans_ref.at[:ranks],
        dst_ref=spans_ref.at[ranks:],
        send_sem=swap_sems.at[0],
        recv_sem=swap_sems.at[1],
        device_id={"batch": 1 - batch_rank},
        device_id_type=MESH,
    )
    swap.start()
    loads[3].wait()
    loads[4].wait()
    start_marks(span_ends(lens_ref, batch_rank), keys, vals, hot, tri, rows_ref, lat)

    def step(g, carry):
        attend_pair(
            g, kw, vw, qs, spans_ref, rows_ref, keys, vals, hot, tri, part_ref, lat, look, scale
        )
        return carry

    lax.fori_loop(0, some // keys.shape[0], step, 0)
    for way, part in streams:
        for t in range(1, hops(way, part) + 1):
            hop(way, part, t).wait_send()
    for give in gives:
        give.wait()
    keep.wait()
    swap.wait()


HBM_SPEC = pl.BlockSpec(memory_space=pltpu.HBM)
VMEM_SPEC = pl.BlockSpec(memory_space=pltpu.VMEM)
SMEM_SPEC = pl.BlockSpec(memory_space=pltpu.SMEM)


def attend_scratch(span_len, kv, lat, qb):
    pair = 2
    marks = 128 - (kv - lat)
    return [
        pltpu.VMEM((pair, span_len, 256), jnp.bfloat16),
        pltpu.VMEM((pair, 128 + 16, span_len), jnp.bfloat16),
        pltpu.VMEM((marks, span_len), jnp.bfloat16),
        pltpu.VMEM((qb, qb), jnp.float32),
    ]


def gather_pallas(lens, shard, flat_queries, key_weight, value_weight, turned, owned, ranks, first, qb):
    heads, width, span_len = turned.shape
    kv, own = shard.shape
    lat = key_weight.shape[0]
    rows = flat_queries.shape[0]
    block = rows // (ranks * owned)
    look = min(-(-(span_len // 2) // qb), span_len // qb - 1)
    bf16 = jnp.bfloat16
    return pl.pallas_call(
        functools.partial(
            gather_kernel,
            lat=lat,
            ranks=ranks,
            heads=heads,
            look=look,
            scale=math.log2(math.e) / math.sqrt(width),
        ),
        out_shape=(
            jax.ShapeDtypeStruct((2 * ranks, kv, own), bf16),
            jax.ShapeDtypeStruct((span_len, kv), bf16),
            jax.ShapeDtypeStruct((ranks, owned, block, kv), bf16),
            jax.ShapeDtypeStruct((span_len, first * 128), bf16),
        ),
        in_specs=[SMEM_SPEC] + [HBM_SPEC] * 5,
        out_specs=(VMEM_SPEC,) * 4,
        scratch_shapes=[
            pltpu.VMEM(key_weight.shape, bf16),
            pltpu.VMEM((lat, first * 128), bf16),
            pltpu.VMEM((first, width, span_len), bf16),
            pltpu.VMEM((rows, width), bf16),
            pltpu.VMEM((rows, 128), jnp.float32),
            pltpu.VMEM((lat // 128, rows, 128), jnp.float32),
            pltpu.VMEM((ranks, owned, block, kv), bf16),
            *attend_scratch(span_len, kv, lat, qb),
            pltpu.SemaphoreType.DMA((6,)),
            pltpu.SemaphoreType.DMA((2, 2, ranks // 2)),
            pltpu.SemaphoreType.DMA((2, 2, ranks // 2)),
            pltpu.SemaphoreType.DMA((2,)),
            pltpu.SemaphoreType.DMA((ranks - 1,)),
            pltpu.SemaphoreType.DMA((ranks - 1,)),
        ],
        compiler_params=pltpu.CompilerParams(
            collective_id=0, has_side_effects=True, vmem_limit_bytes=40 << 20
        ),
        cost_estimate=pl.CostEstimate(
            flops=12 * 10**9, bytes_accessed=12 << 20, transcendentals=6 << 20
        ),
    )(lens, shard, flat_queries, key_weight, value_weight, turned)


def decode_kernel(
    lens_ref, owner_ref, ctx_ref, q_ref, new_ref, spans_ref, part_ref, cache_ref,
    out_ref, whole_ref,
    bufs, sems, whole_sem, m_ref, l_ref, acc_ref,
    *, lat, heads, steps, blk, depth, scale, rows_local, span_len
):
    ranks, owned, block, kv = q_ref.shape
    rows = ranks * block
    batch_rank = lax.axis_index("batch")
    me = lax.axis_index("head")
    shown = pltpu.make_async_copy(
        part_ref, whole_ref.at[:, : part_ref.shape[1]], whole_sem.at[0]
    )
    shown.start()
    facts = []
    for r in range(owned):
        row = batch_rank * rows_local + me * owned + r
        target = jnp.int32(0)
        first = jnp.int32(0)
        length = jnp.int32(0)
        for c in range(lens_ref.shape[0]):
            start = jnp.int32(c * span_len)
            for k in range(lens_ref.shape[1]):
                hit = (owner_ref[c, k] == row).astype(jnp.int32)
                target = target + hit
                first = first + hit * start
                length = length + hit * lens_ref[c, k]
                start = start + lens_ref[c, k]
        first = lax.rem(first + batch_rank * span_len, 2 * span_len) * target
        length = jnp.where(target > 0, length, ctx_ref[r])
        facts.append((target, first, length))

    def copy_of(r, t):
        slot = lax.rem(t, depth)
        target, start, _ = facts[r]
        at = pl.multiple_of(start // blk * blk + t * blk, blk)

        @pl.when(target > 0)
        def _():
            own = spans_ref.shape[2]
            for c in range(blk // own):
                pltpu.make_async_copy(
                    spans_ref.at[at // own + c],
                    bufs.at[r, slot, :, c * own : (c + 1) * own],
                    sems.at[r, slot],
                ).start()

        @pl.when(target == 0)
        def _():
            pltpu.make_async_copy(
                cache_ref.at[r, :, pl.ds(at, blk)], bufs.at[r, slot], sems.at[r, slot]
            ).start()

    counts = []
    for r in range(owned):
        _, start, length = facts[r]
        counts.append((start + length + blk - 1) // blk - start // blk)
    for r in range(owned):
        for t in range(depth - 1):
            pl.when(t < counts[r])(functools.partial(copy_of, r, jnp.int32(t)))
    newest = new_ref[...].astype(jnp.float32)
    for r in range(owned):
        _, start, length = facts[r]
        base = start // blk * blk
        q = q_ref[:, r].reshape(rows, kv)
        fresh = jnp.concatenate(
            [newest[s, r : r + 1] for s in range(steps)]
            + [jnp.zeros((128 - steps, kv), jnp.float32)],
            axis=0,
        ).astype(jnp.bfloat16)
        s = trans_dot(q, fresh)
        row_step = (lax.broadcasted_iota(jnp.int32, s.shape, 0) // heads) % steps
        col = lax.broadcasted_iota(jnp.int32, s.shape, 1)
        s = jnp.where(col <= row_step, s, NEGATIVE)
        m = jnp.max(s, axis=1, keepdims=True)
        w = jnp.exp2((s - m) * scale)
        l_ref[...] = jnp.broadcast_to(jnp.sum(w, axis=1, keepdims=True), l_ref.shape)
        m_ref[...] = jnp.broadcast_to(m, m_ref.shape)
        acc_ref[...] = jnp.dot(
            w.astype(jnp.bfloat16), fresh[:, :lat], preferred_element_type=jnp.float32
        )

        def step(t, carry):
            slot = lax.rem(t, depth)
            pl.when(t + depth - 1 < counts[r])(lambda: copy_of(r, t + depth - 1))
            pltpu.make_async_copy(
                cache_ref.at[r, :, pl.ds(0, blk)], bufs.at[r, slot], sems.at[r, slot]
            ).wait()
            keys = bufs[r, slot]
            s = jnp.dot(q, keys, preferred_element_type=jnp.float32)
            place = base + t * blk + lax.broadcasted_iota(jnp.int32, (1, blk), 1)
            hide = jnp.where((place >= start) & (place < start + length), 0.0, NEGATIVE)
            s = s + hide
            old = m_ref[:, :1]
            new = jnp.maximum(old, jnp.max(s, axis=1, keepdims=True))
            alpha = jnp.exp2((old - new) * scale)
            w = jnp.exp2((s - new) * scale)
            l_new = l_ref[:, :1] * alpha + jnp.sum(w, axis=1, keepdims=True)
            l_ref[...] = jnp.broadcast_to(l_new, l_ref.shape)
            m_ref[...] = jnp.broadcast_to(new, m_ref.shape)
            acc_ref[...] = acc_ref[...] * alpha + trans_dot(w.astype(jnp.bfloat16), keys[:lat])
            return carry

        lax.fori_loop(0, counts[r], step, 0)
        done = (acc_ref[...] / l_ref[:, :1]).astype(out_ref.dtype)
        for p in range(ranks):
            out_ref[p, r] = done[p * block : (p + 1) * block]
    shown.wait()


def decode_pallas(lens, owner, ctx, query, newest, spans, part, cache, lat, heads, all_columns, width, rows_local, blk=512, depth=4):
    ranks, owned, block, kv = query.shape
    rows = ranks * block
    steps = block // heads
    span_len = part.shape[0]
    return pl.pallas_call(
        functools.partial(
            decode_kernel,
            lat=lat,
            heads=heads,
            steps=steps,
            blk=blk,
            depth=depth,
            scale=math.log2(math.e) / math.sqrt(width),
            rows_local=rows_local,
            span_len=span_len,
        ),
        out_shape=(
            jax.ShapeDtypeStruct((ranks, owned, block, lat), jnp.bfloat16),
            jax.ShapeDtypeStruct((span_len, all_columns), jnp.bfloat16),
        ),
        in_specs=[SMEM_SPEC] * 3
        + [VMEM_SPEC, VMEM_SPEC, pl.BlockSpec(memory_space=pl.ANY), VMEM_SPEC, HBM_SPEC],
        out_specs=(VMEM_SPEC, HBM_SPEC),
        scratch_shapes=[
            pltpu.VMEM((owned, depth, kv, blk), jnp.bfloat16),
            pltpu.SemaphoreType.DMA((owned, depth)),
            pltpu.SemaphoreType.DMA((1,)),
            pltpu.VMEM((rows, 128), jnp.float32),
            pltpu.VMEM((rows, 128), jnp.float32),
            pltpu.VMEM((rows, lat), jnp.float32),
        ],
        compiler_params=pltpu.CompilerParams(vmem_limit_bytes=40 << 20),
        cost_estimate=pl.CostEstimate(
            flops=5 * 10**9, bytes_accessed=10 << 20, transcendentals=2 << 20
        ),
    )(lens, owner, ctx, query, newest, spans, part, cache)


def return_kernel(
    lens_ref, rows_ref, spans_ref, lo_ref, kw_hbm, vw_hbm, q_hbm,
    back_ref, part_ref,
    kw, vw, qs, keys, vals, hot, tri, load_sems, give_sems, take_sems,
    *, lat, ranks, look, scale, turn_at
):
    me = lax.axis_index("head")
    batch_rank = lax.axis_index("batch")
    some = qs.shape[0]
    skip = q_hbm.shape[0] - some
    barrier = pltpu.get_barrier_semaphore()
    for k in range(1, ranks):
        pl.semaphore_signal(
            barrier, inc=1, device_id={"head": (me + k) % ranks}, device_id_type=MESH
        )
    loads = [
        pltpu.make_async_copy(kw_hbm.at[:, skip * 128 :], kw, load_sems.at[0]),
        pltpu.make_async_copy(vw_hbm.at[:, skip * 128 :], vw, load_sems.at[1]),
        pltpu.make_async_copy(q_hbm.at[skip:], qs, load_sems.at[2]),
    ]
    for load in loads:
        load.start()
    start_marks(span_ends(lens_ref, batch_rank), keys, vals, hot, tri, rows_ref, lat)
    for load in loads:
        load.wait()
    gives = []
    for k in range(1, ranks):
        peer = (me + k) % ranks
        gives.append(
            pltpu.make_async_remote_copy(
                src_ref=lo_ref.at[peer],
                dst_ref=back_ref.at[me],
                send_sem=give_sems.at[k - 1],
                recv_sem=take_sems.at[k - 1],
                device_id={"head": peer},
                device_id_type=MESH,
            )
        )
    keep = pltpu.make_async_copy(lo_ref.at[me], back_ref.at[me], load_sems.at[3])
    keep.start()

    def step(g, carry):
        @pl.when(g == turn_at)
        def _():
            pl.semaphore_wait(barrier, ranks - 1)
            for give in gives:
                give.start()

        attend_pair(
            g, kw, vw, qs, spans_ref, rows_ref, keys, vals, hot, tri, part_ref, lat, look, scale
        )
        return carry

    lax.fori_loop(0, some // keys.shape[0], step, 0)
    for give in gives:
        give.wait()
    keep.wait()


def return_pallas(lens, rows, spans, latent_out, key_weight, value_weight, turned, rest, qb, turn_at):
    heads, width, span_len = turned.shape
    ranks = latent_out.shape[0]
    lat = key_weight.shape[0]
    kv = rows.shape[1]
    look = min(-(-(span_len // 2) // qb), span_len // qb - 1)
    bf16 = jnp.bfloat16
    return pl.pallas_call(
        functools.partial(
            return_kernel,
            lat=lat,
            ranks=ranks,
            look=look,
            scale=math.log2(math.e) / math.sqrt(width),
            turn_at=turn_at,
        ),
        out_shape=(
            jax.ShapeDtypeStruct(latent_out.shape, bf16),
            jax.ShapeDtypeStruct((span_len, rest * 128), bf16),
        ),
        in_specs=[SMEM_SPEC] + [VMEM_SPEC] * 3 + [HBM_SPEC] * 3,
        out_specs=(VMEM_SPEC,) * 2,
        scratch_shapes=[
            pltpu.VMEM((lat, rest * 128), bf16),
            pltpu.VMEM((lat, rest * 128), bf16),
            pltpu.VMEM((rest, width, span_len), bf16),
            *attend_scratch(span_len, kv, lat, qb),
            pltpu.SemaphoreType.DMA((4,)),
            pltpu.SemaphoreType.DMA((ranks - 1,)),
            pltpu.SemaphoreType.DMA((ranks - 1,)),
        ],
        compiler_params=pltpu.CompilerParams(
            collective_id=1, has_side_effects=True, vmem_limit_bytes=40 << 20
        ),
        cost_estimate=pl.CostEstimate(
            flops=12 * 10**9, bytes_accessed=12 << 20, transcendentals=6 << 20
        ),
    )(lens, rows, spans, latent_out, key_weight, value_weight, turned)


def project_kernel(back_ref, vw_ref, part_ref, half_ref, out_ref, whole_ref, wide, sems, *, heads, lat):
    ranks, owned, block, _ = back_ref.shape
    steps = block // heads
    local = ranks * owned
    columns = part_ref.shape[1]
    shown = pltpu.make_async_copy(
        part_ref, whole_ref.at[:, whole_ref.shape[1] - columns :], sems.at[0]
    )
    shown.start()
    for p in range(ranks):
        for r in range(owned):
            at = (p * owned + r) * block
            for c in range(lat // 128):
                wide[c, at : at + block] = back_ref[p, r, :, c * 128 : (c + 1) * 128].astype(
                    jnp.float32
                )
    for h in range(heads):
        mine = jnp.concatenate(
            [
                jnp.concatenate(
                    [
                        wide[c, pl.ds(s * heads + h, local, stride=block), :]
                        for c in range(lat // 128)
                    ],
                    axis=1,
                )
                for s in range(steps)
            ],
            axis=0,
        ).astype(jnp.bfloat16)
        out_ref[:, h * 128 : (h + 1) * 128] = jnp.dot(
            mine, vw_ref[:, h * 128 : (h + 1) * 128], preferred_element_type=jnp.float32
        ).astype(jnp.bfloat16)
    shown.wait()


def project_pallas(back, value_weight, part, whole, heads):
    ranks, owned, block, lat = back.shape
    rows = ranks * owned * block
    return pl.pallas_call(
        functools.partial(project_kernel, heads=heads, lat=lat),
        out_shape=(
            jax.ShapeDtypeStruct((rows // heads, heads * 128), jnp.bfloat16),
            jax.ShapeDtypeStruct(whole.shape, whole.dtype),
        ),
        in_specs=[VMEM_SPEC, VMEM_SPEC, VMEM_SPEC, HBM_SPEC],
        out_specs=(VMEM_SPEC, HBM_SPEC),
        scratch_shapes=[
            pltpu.VMEM((lat // 128, rows, 128), jnp.float32),
            pltpu.SemaphoreType.DMA((1,)),
        ],
        input_output_aliases={3: 1},
        compiler_params=pltpu.CompilerParams(vmem_limit_bytes=24 << 20),
    )(back, value_weight, part, whole)


def on_device(
    latent_rows,
    pre_queries,
    pre_lengths,
    owner_map,
    context_cache,
    context_lengths,
    new_latent,
    dec_queries,
    key_weight,
    value_weight,
):
    steps, rows_local, heads, width = dec_queries.shape
    ranks = lax.axis_size("head")
    if heads % 16 or latent_rows.shape[0] % 128 or ranks % 2:
        return plain_on_device(
            latent_rows,
            pre_queries,
            pre_lengths,
            owner_map,
            context_cache,
            context_lengths,
            new_latent,
            dec_queries,
            key_weight,
            value_weight,
        )
    lat = key_weight.shape[0]
    owned = context_cache.shape[0]
    first = heads // 2
    qb = 256
    turned = jnp.transpose(pre_queries, (1, 2, 0))
    spans, rows, query, part = gather_pallas(
        pre_lengths,
        jnp.transpose(latent_rows),
        dec_queries.reshape(-1, width),
        key_weight,
        value_weight,
        turned,
        owned,
        ranks,
        first,
        qb,
    )
    latent_out, whole = decode_pallas(
        pre_lengths,
        owner_map,
        context_lengths,
        query,
        new_latent,
        spans,
        part,
        jnp.transpose(context_cache, (0, 2, 1)),
        lat,
        heads,
        heads * 128,
        width,
        rows_local,
    )
    back, rest = return_pallas(
        pre_lengths, rows, spans, latent_out, key_weight, value_weight, turned, heads - first, qb, 1
    )
    decode_out, prefill_out = project_pallas(back, value_weight, rest, whole, heads)
    return (prefill_out, decode_out.reshape(steps, rows_local, heads * 128))


def solution(mesh):
    placed = (
        P(("groups", "batch", "head"), None),
        P(("groups", "batch"), "head", None),
        P("groups", None),
        P("groups", None),
        P(("groups", "batch", "head"), None, None),
        P(("groups", "batch", "head")),
        P("groups", ("batch", "head"), None),
        P("groups", "batch", "head", None),
        P(None, "head"),
        P(None, "head"),
    )
    return jax.shard_map(
        on_device,
        mesh=mesh,
        in_specs=placed,
        out_specs=(P(("groups", "batch"), "head"), P("groups", "batch", "head")),
        check_vma=False,
    )
```

time: 166 us -> 83 us (0.50)
  the two profiles are of different devices: /device:TPU:0 before, /device:TPU:10 now
where the time goes in v1:
time: 83 us; the launch traced here: 81.5 us
  Pallas kernels  74.9 us (90%)
  local copies, waits for them, and re-layouts  5.74 us (7%)
  between operations  0.89 us (1%)
    pallas_call x1, Pallas kernels, gather_pallas(): pl.pallas_call(functools.partial(gather_kernel, lat=lat, ranks=ranks, hea...  41.4 us
    pallas_call x1, Pallas kernels, return_pallas(): pl.pallas_call(functools.partial(return_kernel, lat=lat, ranks=ranks, loo...  20 us
    pallas_call x1, Pallas kernels, decode_pallas(): pl.pallas_call(functools.partial(decode_kernel, lat=lat, heads=heads, ste...  10.3 us
    unnamed x20, local copies, waits for them, and re-layouts  5.74 us
    pallas_call x1, Pallas kernels, project_pallas(): pl.pallas_call(functools.partial(project_kernel, heads=heads, lat=lat), o...  3.13 us

profile of v1, /device:TPU:10, one launch (start us, length us, event | category | flops | bytes accessed | tf_op | source)
XLA Modules:
  0.0 81.5 jit_solution(18164535291030422696)
XLA Ops:
  0.6 0.0 copy-start
  0.6 1.6 %copy-done = bf16[512,2048]{1,0:T(8,128)(2,1)S(1)} copy-done((bf16[512,2048]{1,0:T(8,128)(2,1)S(1)}, bf16[512,2048]{1,0:T(8,128)(2,1)}, u32[]{:S(2)}) %copy-start) | copy-done | bytes 2097176
  2.2 0.0 copy-start.2
  2.2 1.6 %copy-done.2 = bf16[512,2048]{1,0:T(8,128)(2,1)S(1)} copy-done((bf16[512,2048]{1,0:T(8,128)(2,1)S(1)}, bf16[512,2048]{1,0:T(8,128)(2,1)}, u32[]{:S(2)}) %copy-start.2) | copy-done | bytes 2097176
  3.8 0.0 copy-start.4
  3.8 0.9 %copy-done.4 = bf16[2,16,16,192]{3,2,1,0:T(8,128)(2,1)S(1)} copy-done((bf16[2,16,16,192]{3,2,1,0:T(8,128)(2,1)S(1)}, bf16[2,16,16,192]{3,2,1,0:T(8,128)(2,1)}, u32[]{:S(2)}) %copy-start.4) | copy-done | bytes 196632
  4.8 0.0 copy-start.5
  4.8 0.9 %copy-done.5 = bf16[128,576]{0,1:T(8,128)(2,1)S(1)} copy-done((bf16[128,576]{0,1:T(8,128)(2,1)S(1)}, bf16[128,576]{0,1:T(8,128)(2,1)}, u32[]{:S(2)}) %copy-start.5) | copy-done | bytes 147480
  5.7 0.0 copy-start.8
  5.7 0.7 copy-done.8
  6.4 0.0 copy-start.6
  6.4 0.0 copy-start.7
  6.4 0.0 copy-start.9
  6.4 41.4 %shard_map.113 = (bf16[16,576,128]{2,1,0:T(8,128)(2,1)S(1)}, bf16[1024,576]{1,0:T(8,128)(2,1)S(1)}, bf16[8,2,32,576]{3,2,1,0:T(8,128)(2,1)S(1)}, bf16[1024,1024]{1,0:T(8,128)(2,1)S(1)}) custom-call(s32[2,4]{1,0:T(2,128)S(1)} %copy-done.8, bf16[576,128]{1,0:T(8,128)(2,1)S(1)} %bitcast.6, bf16[512,192]{1,0:T(8,128)(2,1)S(1)} %bitcast.5, ...), custom_call_target="tpu_custom_call" | custom-call | flops 12000000000 | bytes 12582912 | tf_op jit(solution)/shard_map/pallas_call | solution.py:448
  47.8 0.0 copy-done.6
  47.8 0.0 copy-done.7
  47.8 0.0 copy-done.9
  47.8 0.0 copy-start.1
  47.8 0.0 copy-start.3
  47.9 10.3 %shard_map.114 = (bf16[8,2,32,512]{3,2,1,0:T(8,128)(2,1)S(1)}, bf16[1024,2048]{1,0:T(8,128)(2,1)}) custom-call(s32[2,4]{1,0:T(2,128)S(1)} %copy-done.8, s32[2,4]{1,0:T(2,128)S(1)} %copy-done.7, s32[2]{0:T(128)S(1)} %copy-done.9, bf16[8,2,32,576]{3,2,1,0:T(8,128)(2,1)S(1)} %get-tuple-element.14.q_ref, bf16[2,2,576]{2,1,0:T(2,128)(2,1)S(1)} %copy-done.6, ...), custom_call_target="tpu_custom_call" | custom-call | flops 5000000000 | bytes 10485760 | tf_op jit(solution)/shard_map/pallas_call | solution.py:605
  58.2 0.0 copy-done.1
  58.2 0.0 copy-done.3
  58.2 20.0 %shard_map.115 = (bf16[8,2,32,512]{3,2,1,0:T(8,128)(2,1)S(1)}, bf16[1024,1024]{1,0:T(8,128)(2,1)S(1)}) custom-call(s32[2,4]{1,0:T(2,128)S(1)} %copy-done.8, bf16[1024,576]{1,0:T(8,128)(2,1)S(1)} %get-tuple-element.12.rows_ref, bf16[16,576,128]{2,1,0:T(8,128)(2,1)S(1)} %get-tuple-element.13.spans_ref, bf16[8,2,32,512]{3,2,1,0:T(8,128)(2,1)S(1)} %get-tuple-element.16.lo_ref, ...), custom_call_target="tpu_custom_call" | custom-call | flops 12000000000 | bytes 12582912 | tf_op jit(solution)/shard_map/pallas_call | solution.py:705
  78.2 3.1 %shard_map.116 = (bf16[32,2048]{1,0:T(8,128)(2,1)}, bf16[1024,2048]{1,0:T(8,128)(2,1)}) custom-call(bf16[8,2,32,512]{3,2,1,0:T(8,128)(2,1)S(1)} %get-tuple-element.17.back_ref, bf16[512,2048]{1,0:T(8,128)(2,1)S(1)} %copy-done.1, bf16[1024,1024]{1,0:T(8,128)(2,1)S(1)} %get-tuple-element.18.part_ref, ...), custom_call_target="tpu_custom_call", output_to_operand_aliasing={{1}: (3, {})} | custom-call | tf_op jit(solution)/shard_map/pallas_call | solution.py:777
Async XLA Ops:
  0.6 1.6 %copy-start = (bf16[512,2048]{1,0:T(8,128)(2,1)S(1)}, bf16[512,2048]{1,0:T(8,128)(2,1)}, u32[]{:S(2)}) copy-start(bf16[512,2048]{1,0:T(8,128)(2,1)} %vw_ref.1) | copy-start | bytes 6291460
  2.2 1.6 %copy-start.2 = (bf16[512,2048]{1,0:T(8,128)(2,1)S(1)}, bf16[512,2048]{1,0:T(8,128)(2,1)}, u32[]{:S(2)}) copy-start(bf16[512,2048]{1,0:T(8,128)(2,1)} %kw_hbm.3) | copy-start | bytes 6291460
  3.8 0.9 %copy-start.4 = (bf16[2,16,16,192]{3,2,1,0:T(8,128)(2,1)S(1)}, bf16[2,16,16,192]{3,2,1,0:T(8,128)(2,1)}, u32[]{:S(2)}) copy-start(bf16[2,16,16,192]{3,2,1,0:T(8,128)(2,1)} %param.17) | copy-start | bytes 589828
  4.8 0.9 %copy-start.5 = (bf16[128,576]{0,1:T(8,128)(2,1)S(1)}, bf16[128,576]{0,1:T(8,128)(2,1)}, u32[]{:S(2)}) copy-start(bf16[128,576]{0,1:T(8,128)(2,1)} %param.10) | copy-start | bytes 442372
  5.7 0.7 copy-start.8
  6.4 41.4 %copy-start.6 = (bf16[2,2,576]{2,1,0:T(2,128)(2,1)S(1)}, bf16[2,2,576]{2,1,0:T(2,128)(2,1)}, u32[]{:S(2)}) copy-start(bf16[2,2,576]{2,1,0:T(2,128)(2,1)} %new_ref.1) | copy-start | bytes 13828
  6.4 41.4 %copy-start.7 = (s32[2,4]{1,0:T(2,128)S(1)}, s32[2,4]{1,0:T(2,128)}, u32[]{:S(2)}) copy-start(s32[2,4]{1,0:T(2,128)} %owner_ref.1) | copy-start | bytes 100
  6.4 41.5 %copy-start.9 = (s32[2]{0:T(128)S(1)}, s32[2]{0:T(128)}, u32[]{:S(2)}) copy-start(s32[2]{0:T(128)} %ctx_ref.1) | copy-start | bytes 28
  47.8 10.4 %copy-start.1 = (bf16[512,2048]{1,0:T(8,128)(2,1)S(1)}, bf16[512,2048]{1,0:T(8,128)(2,1)}, u32[]{:S(2)}) copy-start(bf16[512,2048]{1,0:T(8,128)(2,1)} %vw_ref.1) | copy-start | bytes 6291460
  47.8 10.4 %copy-start.3 = (bf16[512,2048]{1,0:T(8,128)(2,1)S(1)}, bf16[512,2048]{1,0:T(8,128)(2,1)}, u32[]{:S(2)}) copy-start(bf16[512,2048]{1,0:T(8,128)(2,1)} %kw_hbm.3) | copy-start | bytes 6291460

commit v2 on v1

--- a/solution.py
+++ b/solution.py
@@ -202,10 +202,10 @@
     return (1 - late) * (2 * place) + late * (2 * (ranks - 1 - place) + 1)
 
 
-def start_marks(ends, keys, vals, hot, tri, rows_ref, lat):
-    pair, span_len, _ = keys.shape
+def start_marks(ends, both_keys, both_vals, hot, tri, rows_ref, lat):
+    pair, span_len, full = both_keys[0].shape
     segs = len(ends)
-    marks = keys.shape[2] - 128 - (rows_ref.shape[1] - lat)
+    marks = full - 128 - (rows_ref.shape[1] - lat)
     where = lax.broadcasted_iota(jnp.int32, (span_len, marks), 0)
     lane = lax.broadcasted_iota(jnp.int32, (span_len, marks), 1)
     place = lax.broadcasted_iota(jnp.int32, (marks, span_len), 1)
@@ -217,49 +217,158 @@
         seen = seen + (place >= ends[k]).astype(jnp.int32)
     mark = jnp.where((lane < segs) & (lane != mine), NEGATIVE, 0.0).astype(jnp.bfloat16)
     hot[...] = jnp.where(line == seen, 1.0, 0.0).astype(jnp.bfloat16)
-    for p in range(pair):
-        keys[p, :, 128 : keys.shape[2] - marks] = rows_ref[:, lat:]
-        keys[p, :, keys.shape[2] - marks :] = mark
-        vals[p, 128:, :] = jnp.ones((vals.shape[1] - 128, span_len), jnp.bfloat16)
+    for keys, vals in zip(both_keys, both_vals):
+        for p in range(pair):
+            keys[p, :, 128 : full - marks] = rows_ref[:, lat:]
+            keys[p, :, full - marks :] = mark
+            vals[p, 128:, :] = jnp.ones((vals.shape[1] - 128, span_len), jnp.bfloat16)
     size = tri.shape[0]
     key_at = lax.broadcasted_iota(jnp.int32, (size, size), 0)
     query_at = lax.broadcasted_iota(jnp.int32, (size, size), 1)
     tri[...] = jnp.where(key_at <= query_at, 0.0, NEGATIVE)
 
 
-def attend_pair(g, kw, vw, qs, spans_ref, rows_ref, keys, vals, hot, tri, part_ref, lat, look, scale):
+def value_piece(c, turned, spans_ref, vals, lat):
+    latents = jnp.concatenate([spans_ref[2 * c, :lat, :], spans_ref[2 * c + 1, :lat, :]], axis=1)
+    value = jnp.dot(turned[...], latents, preferred_element_type=jnp.float32).astype(jnp.bfloat16)
+    for p in range(vals.shape[0]):
+        vals[p, :128, c * 256 : (c + 1) * 256] = value[p * 128 : (p + 1) * 128]
+
+
+def key_piece(rows, columns, kw, rows_ref, keys, lat):
+    made = jnp.dot(rows_ref[rows, :lat], kw[:, columns], preferred_element_type=jnp.float32)
+    made = made.astype(jnp.bfloat16)
+    for p in range(keys.shape[0]):
+        keys[p, rows, :128] = made[:, p * 128 : (p + 1) * 128]
+
+
+def projections(g, kw, vw, spans_ref, rows_ref, turned, keys, vals, lat):
+    pair, span_len, _ = keys.shape
+    wide = pair * 128
+    columns = pl.ds(pl.multiple_of(g * wide, wide), wide)
+
+    def turn():
+        turned[...] = jnp.transpose(vw[:, columns])
+
+    half = span_len // 2
+    pieces = [turn]
+    for k in range(2):
+        rows = slice(k * half, (k + 1) * half)
+        pieces.append(functools.partial(key_piece, rows, columns, kw, rows_ref, keys, lat))
+    for c in range(span_len // 256):
+        pieces.append(functools.partial(value_piece, c, turned, spans_ref, vals, lat))
+    return pieces
+
+
+def attention(g, qs, keys, vals, hot, tri, part_ref, scores, weights, look, scale, others):
     pair, span_len, _ = keys.shape
     qb = tri.shape[0]
-    wide = pair * 128
-    columns = pl.ds(pl.multiple_of(g * wide, wide), wide)
-    made = jnp.dot(rows_ref[:, :lat], kw[:, columns], preferred_element_type=jnp.float32)
-    made = made.astype(jnp.bfloat16)
-    for p in range(pair):
-        keys[p, :, :128] = made[:, p * 128 : (p + 1) * 128]
-    turned = jnp.transpose(vw[:, columns])
-    for c in range(span_len // 256):
-        latents = jnp.concatenate(
-            [spans_ref[2 * c, :lat, :], spans_ref[2 * c + 1, :lat, :]], axis=1
-        )
-        value = jnp.dot(turned, latents, preferred_element_type=jnp.float32).astype(jnp.bfloat16)
-        for p in range(pair):
-            vals[p, :128, c * 256 : (c + 1) * 256] = value[p * 128 : (p + 1) * 128]
-    for i in range(span_len // qb):
-        lo, hi = max(i - look, 0) * qb, (i + 1) * qb
-        for p in range(pair):
-            query = jnp.concatenate(
-                [qs[g * pair + p, :, i * qb : hi], hot[:, i * qb : hi]], axis=0
+    blocks = span_len // qb
+    order = [(0, 0)] + [(i, p) for i in range(1, blocks) for p in range(pair)]
+    order += [(0, p) for p in range(1, pair)]
+    count = len(order)
+    lengths = [min(i, look) + 1 for i, _ in order]
+    peaks = [None] * count
+    tops = [None] * count
+    sums = [None] * count
+
+    def score(n, c):
+        i, p = order[n]
+        at = (i - lengths[n] + 1 + c) * qb
+        query = jnp.concatenate(
+            [qs[g * pair + p, :, i * qb : (i + 1) * qb], hot[:, i * qb : (i + 1) * qb]], axis=0
+        )
+        s = jnp.dot(keys[p, at : at + qb, :], query, preferred_element_type=jnp.float32)
+        if c == lengths[n] - 1:
+            s = s + tri[...]
+        scores[n % 2][c * qb : (c + 1) * qb, :] = s
+        top = jnp.max(s.reshape(qb // 8, 8, qb), axis=0)
+        peaks[n] = top if peaks[n] is None else jnp.maximum(peaks[n], top)
+
+    def soften(n, c):
+        if c == 0:
+            tops[n] = jnp.max(peaks[n], axis=0, keepdims=True)
+        s = scores[n % 2][c * qb : (c + 1) * qb, :]
+        w = jnp.exp2((s - tops[n]) * scale)
+        weights[n % 2][c * qb : (c + 1) * qb, :] = w.astype(jnp.bfloat16)
+
+    def mix(n, c):
+        i, p = order[n]
+        at = (i - lengths[n] + 1 + c) * qb
+        o = jnp.dot(
+            vals[p, :, at : at + qb],
+            weights[n % 2][c * qb : (c + 1) * qb, :],
+            preferred_element_type=jnp.float32,
+        )
+        sums[n] = o if sums[n] is None else sums[n] + o
+        if c == lengths[n] - 1:
+            o = sums[n]
+            o = o[:128] * (1.0 / o[128:129])
+            columns = pl.ds(pl.multiple_of((g * pair + p) * 128, 128), 128)
+            part_ref[i * qb : (i + 1) * qb, columns] = jnp.transpose(o.astype(jnp.bfloat16))
+
+    todo_score = [(n, c) for n in range(count) for c in range(lengths[n])]
+    todo_soft = list(todo_score)
+    todo_mix = list(todo_score)
+    total = len(todo_score)
+    scored = [0] * count
+    softened = [0] * count
+    mixed = [0] * count
+    others = list(others)
+    every = total / max(len(others), 1)
+    done = 0
+    step = 0
+    while todo_mix:
+        was = list(softened)
+        if todo_score:
+            n, c = todo_score[0]
+            if n < 2 or softened[n - 2] == lengths[n - 2]:
+                score(n, c)
+                scored[n] += 1
+                todo_score.pop(0)
+        if todo_soft:
+            n, c = todo_soft[0]
+            free = n < 2 or mixed[n - 2] == lengths[n - 2]
+            if scored[n] == lengths[n] and free and not (todo_score and todo_score[0][0] <= n):
+                soften(n, c)
+                softened[n] += 1
+                todo_soft.pop(0)
+        n, c = todo_mix[0]
+        if c < was[n]:
+            mix(n, c)
+            mixed[n] += 1
+            todo_mix.pop(0)
+        step += 1
+        while done < len(others) and done * every <= step - 1:
+            others[done]()
+            done += 1
+    while done < len(others):
+        others[done]()
+        done += 1
+
+
+def attend_all(turns, tools, shared, before):
+    kw, vw, qs, spans_ref, rows_ref, part_ref, lat, look, scale = shared
+    keys, vals, hot, tri, turned, scores, weights = tools
+    for piece in projections(0, kw, vw, spans_ref, rows_ref, turned[0], keys[0], vals[0], lat):
+        piece()
+
+    def step(j, carry):
+        before(j)
+        for side in range(2):
+            g = 2 * j + side
+            following = jnp.minimum(g + 1, 2 * turns - 1)
+            others = projections(
+                following, kw, vw, spans_ref, rows_ref,
+                turned[1 - side], keys[1 - side], vals[1 - side], lat,
             )
-            s = jnp.dot(keys[p, lo:hi, :], query, preferred_element_type=jnp.float32)
-            last = s[hi - lo - qb :] + tri[...]
-            s = last if hi - lo == qb else jnp.concatenate([s[: hi - lo - qb], last], axis=0)
-            m = jnp.max(s, axis=0, keepdims=True)
-            w = jnp.exp2((s - m) * scale).astype(jnp.bfloat16)
-            o = jnp.dot(vals[p, :, lo:hi], w, preferred_element_type=jnp.float32)
-            o = o[:128] * (1.0 / o[128:129])
-            part_ref[i * qb : hi, pl.ds(pl.multiple_of(g * wide + p * 128, 128), 128)] = (
-                jnp.transpose(o.astype(jnp.bfloat16))
+            attention(
+                g, qs, keys[side], vals[side], hot, tri, part_ref,
+                scores, weights, look, scale, others,
             )
+        return carry
+
+    lax.fori_loop(0, turns, step, 0)
 
 
 def absorb_into(dq, kw, sent, flat, wide, heads, lat):
@@ -300,7 +409,7 @@
 def gather_kernel(
     lens_ref, shard_hbm, dq_hbm, kw_hbm, vw_hbm, q_hbm,
     spans_ref, rows_ref, got_ref, part_ref,
-    kw, vw, qs, dq, flat, wide, sent, keys, vals, hot, tri,
+    kw, vw, qs, dq, flat, wide, sent, tools,
     load_sems, ring_send, ring_recv, swap_sems, give_sems, take_sems,
     *, lat, ranks, heads, look, scale
 ):
@@ -403,15 +512,11 @@
     swap.start()
     loads[3].wait()
     loads[4].wait()
+    keys, vals, hot, tri = tools[:4]
     start_marks(span_ends(lens_ref, batch_rank), keys, vals, hot, tri, rows_ref, lat)
 
-    def step(g, carry):
-        attend_pair(
-            g, kw, vw, qs, spans_ref, rows_ref, keys, vals, hot, tri, part_ref, lat, look, scale
-        )
-        return carry
-
-    lax.fori_loop(0, some // keys.shape[0], step, 0)
+    shared = (kw, vw, qs, spans_ref, rows_ref, part_ref, lat, look, scale)
+    attend_all(some // 4, tools, shared, lambda j: None)
     for way, part in streams:
         for t in range(1, hops(way, part) + 1):
             hop(way, part, t).wait_send()
@@ -426,14 +531,19 @@
 SMEM_SPEC = pl.BlockSpec(memory_space=pltpu.SMEM)
 
 
-def attend_scratch(span_len, kv, lat, qb):
+def attend_scratch(span_len, kv, lat, qb, look):
     pair = 2
     marks = 128 - (kv - lat)
+    bf16 = jnp.bfloat16
+    twice = lambda shape, dtype: [pltpu.VMEM(shape, dtype)] * 2
     return [
-        pltpu.VMEM((pair, span_len, 256), jnp.bfloat16),
-        pltpu.VMEM((pair, 128 + 16, span_len), jnp.bfloat16),
-        pltpu.VMEM((marks, span_len), jnp.bfloat16),
+        twice((pair, span_len, 256), bf16),
+        twice((pair, 128 + 16, span_len), bf16),
+        pltpu.VMEM((marks, span_len), bf16),
         pltpu.VMEM((qb, qb), jnp.float32),
+        twice((pair * 128, lat), bf16),
+        twice(((look + 1) * qb, qb), jnp.float32),
+        twice(((look + 1) * qb, qb), bf16),
     ]
 
 
@@ -470,7 +580,7 @@
             pltpu.VMEM((rows, 128), jnp.float32),
             pltpu.VMEM((lat // 128, rows, 128), jnp.float32),
             pltpu.VMEM((ranks, owned, block, kv), bf16),
-            *attend_scratch(span_len, kv, lat, qb),
+            attend_scratch(span_len, kv, lat, qb, look),
             pltpu.SemaphoreType.DMA((6,)),
             pltpu.SemaphoreType.DMA((2, 2, ranks // 2)),
             pltpu.SemaphoreType.DMA((2, 2, ranks // 2)),
@@ -639,7 +749,7 @@
 def return_kernel(
     lens_ref, rows_ref, spans_ref, lo_ref, kw_hbm, vw_hbm, q_hbm,
     back_ref, part_ref,
-    kw, vw, qs, keys, vals, hot, tri, load_sems, give_sems, take_sems,
+    kw, vw, qs, tools, load_sems, give_sems, take_sems,
     *, lat, ranks, look, scale, turn_at
 ):
     me = lax.axis_index("head")
@@ -658,6 +768,7 @@
     ]
     for load in loads:
         load.start()
+    keys, vals, hot, tri = tools[:4]
     start_marks(span_ends(lens_ref, batch_rank), keys, vals, hot, tri, rows_ref, lat)
     for load in loads:
         load.wait()
@@ -677,19 +788,15 @@
     keep = pltpu.make_async_copy(lo_ref.at[me], back_ref.at[me], load_sems.at[3])
     keep.start()
 
-    def step(g, carry):
-        @pl.when(g == turn_at)
+    def before(j):
+        @pl.when(j == turn_at)
         def _():
             pl.semaphore_wait(barrier, ranks - 1)
             for give in gives:
                 give.start()
 
-        attend_pair(
-            g, kw, vw, qs, spans_ref, rows_ref, keys, vals, hot, tri, part_ref, lat, look, scale
-        )
-        return carry
-
-    lax.fori_loop(0, some // keys.shape[0], step, 0)
+    shared = (kw, vw, qs, spans_ref, rows_ref, part_ref, lat, look, scale)
+    attend_all(some // 4, tools, shared, before)
     for give in gives:
         give.wait()
     keep.wait()
@@ -721,7 +828,7 @@
             pltpu.VMEM((lat, rest * 128), bf16),
             pltpu.VMEM((lat, rest * 128), bf16),
             pltpu.VMEM((rest, width, span_len), bf16),
-            *attend_scratch(span_len, kv, lat, qb),
+            attend_scratch(span_len, kv, lat, qb, look),
             pltpu.SemaphoreType.DMA((4,)),
             pltpu.SemaphoreType.DMA((ranks - 1,)),
             pltpu.SemaphoreType.DMA((ranks - 1,)),
@@ -822,13 +929,15 @@
     owned = context_cache.shape[0]
     first = heads // 2
     qb = 256
-    turned = jnp.transpose(pre_queries, (1, 2, 0))
+    stay = lambda x: pltpu.with_memory_space_constraint(x, pltpu.HBM)
+    turned = stay(jnp.transpose(pre_queries, (1, 2, 0)))
+    kw_stay, vw_stay = stay(key_weight), stay(value_weight)
     spans, rows, query, part = gather_pallas(
         pre_lengths,
-        jnp.transpose(latent_rows),
-        dec_queries.reshape(-1, width),
-        key_weight,
-        value_weight,
+        stay(jnp.transpose(latent_rows)),
+        stay(dec_queries.reshape(-1, width)),
+        kw_stay,
+        vw_stay,
         turned,
         owned,
         ranks,
@@ -843,7 +952,7 @@
         new_latent,
         spans,
         part,
-        jnp.transpose(context_cache, (0, 2, 1)),
+        stay(jnp.transpose(context_cache, (0, 2, 1))),
         lat,
         heads,
         heads * 128,
@@ -851,7 +960,7 @@
         rows_local,
     )
     back, rest = return_pallas(
-        pre_lengths, rows, spans, latent_out, key_weight, value_weight, turned, heads - first, qb, 1
+        pre_lengths, rows, spans, latent_out, kw_stay, vw_stay, turned, heads - first, qb, 0
     )
     decode_out, prefill_out = project_pallas(back, value_weight, rest, whole, heads)
     return (prefill_out, decode_out.reshape(steps, rows_local, heads * 128))

time: 83 us -> 67 us (0.81)
  the two profiles are of different devices: /device:TPU:10 before, /device:TPU:31 now
where the time goes in v2:
time: 67 us; the launch traced here: 67.8 us
  Pallas kernels  66.3 us (99%)
  between operations  0.87 us (1%)
  local copies, waits for them, and re-layouts  0.69 us (1%)
    pallas_call x1, Pallas kernels, gather_pallas(): pl.pallas_call(functools.partial(gather_kernel, lat=lat, ranks=ranks, hea...  29.9 us
    pallas_call x1, Pallas kernels, return_pallas(): pl.pallas_call(functools.partial(return_kernel, lat=lat, ranks=ranks, loo...  22.7 us
    pallas_call x1, Pallas kernels, decode_pallas(): pl.pallas_call(functools.partial(decode_kernel, lat=lat, heads=heads, ste...  10.5 us
    pallas_call x1, Pallas kernels, project_pallas(): pl.pallas_call(functools.partial(project_kernel, heads=heads, lat=lat), o...  3.13 us

profile of v2, /device:TPU:31, one launch (start us, length us, event | category | flops | bytes accessed | tf_op | source)
XLA Modules:
  0.0 67.8 jit_solution(6039192069582735539)
XLA Ops:
  0.6 0.0 copy-start.3
  0.6 0.7 copy-done.3
  1.3 0.0 copy-start.1
  1.3 0.0 copy-start.2
  1.3 0.0 copy-start.4
  1.3 29.9 %shard_map.113 = (bf16[16,576,128]{2,1,0:T(8,128)(2,1)S(1)}, bf16[1024,576]{1,0:T(8,128)(2,1)S(1)}, bf16[8,2,32,576]{3,2,1,0:T(8,128)(2,1)S(1)}, bf16[1024,1024]{1,0:T(8,128)(2,1)S(1)}) custom-call(s32[2,4]{1,0:T(2,128)S(1)} %copy-done.3, bf16[576,128]{1,0:T(8,128)(2,1)} %bitcast.9, bf16[512,192]{1,0:T(8,128)(2,1)} %bitcast.8, bf16[512,2048]{1,0:T(8,128)(2,1)} %kw_hbm.3, ...), custom_call_target="tpu_custom_call" | custom-call | flops 12000000000 | bytes 12582912 | tf_op jit(solution)/shard_map/pallas_call | solution.py:558
  31.2 0.0 copy-done.1
  31.2 0.0 copy-done.2
  31.2 0.0 copy-done.4
  31.2 10.5 %shard_map.114 = (bf16[8,2,32,512]{3,2,1,0:T(8,128)(2,1)S(1)}, bf16[1024,2048]{1,0:T(8,128)(2,1)}) custom-call(s32[2,4]{1,0:T(2,128)S(1)} %copy-done.3, s32[2,4]{1,0:T(2,128)S(1)} %copy-done.2, s32[2]{0:T(128)S(1)} %copy-done.4, bf16[8,2,32,576]{3,2,1,0:T(8,128)(2,1)S(1)} %get-tuple-element.14.q_ref, bf16[2,2,576]{2,1,0:T(2,128)(2,1)S(1)} %copy-done.1, ...), custom_call_target="tpu_custom_call" | custom-call | flops 5000000000 | bytes 10485760 | tf_op jit(solution)/shard_map/pallas_call | solution.py:715
  41.8 0.0 copy-start
  41.8 22.7 %shard_map.115 = (bf16[8,2,32,512]{3,2,1,0:T(8,128)(2,1)S(1)}, bf16[1024,1024]{1,0:T(8,128)(2,1)S(1)}) custom-call(s32[2,4]{1,0:T(2,128)S(1)} %copy-done.3, bf16[1024,576]{1,0:T(8,128)(2,1)S(1)} %get-tuple-element.12.rows_ref, bf16[16,576,128]{2,1,0:T(8,128)(2,1)S(1)} %get-tuple-element.13.spans_ref, bf16[8,2,32,512]{3,2,1,0:T(8,128)(2,1)S(1)} %get-tuple-element.16.lo_ref, ...), custom_call_target="tpu_custom_call" | custom-call | flops 12000000000 | bytes 12582912 | tf_op jit(solution)/shard_map/pallas_call | solution.py:812
  64.5 0.0 copy-done
  64.5 3.1 %shard_map.116 = (bf16[32,2048]{1,0:T(8,128)(2,1)}, bf16[1024,2048]{1,0:T(8,128)(2,1)}) custom-call(bf16[8,2,32,512]{3,2,1,0:T(8,128)(2,1)S(1)} %get-tuple-element.17.back_ref, bf16[512,2048]{1,0:T(8,128)(2,1)S(1)} %copy-done, bf16[1024,1024]{1,0:T(8,128)(2,1)S(1)} %get-tuple-element.18.part_ref, ...), custom_call_target="tpu_custom_call", output_to_operand_aliasing={{1}: (3, {})} | custom-call | tf_op jit(solution)/shard_map/pallas_call | solution.py:884
Async XLA Ops:
  0.6 0.7 %copy-start.3 = (s32[2,4]{1,0:T(2,128)S(1)}, s32[2,4]{1,0:T(2,128)}, u32[]{:S(2)}) copy-start(s32[2,4]{1,0:T(2,128)} %lens_ref.5) | copy-start | bytes 100
  1.3 29.9 %copy-start.1 = (bf16[2,2,576]{2,1,0:T(2,128)(2,1)S(1)}, bf16[2,2,576]{2,1,0:T(2,128)(2,1)}, u32[]{:S(2)}) copy-start(bf16[2,2,576]{2,1,0:T(2,128)(2,1)} %new_ref.1) | copy-start | bytes 13828
  1.3 29.9 %copy-start.2 = (s32[2,4]{1,0:T(2,128)S(1)}, s32[2,4]{1,0:T(2,128)}, u32[]{:S(2)}) copy-start(s32[2,4]{1,0:T(2,128)} %owner_ref.1) | copy-start | bytes 100
  1.3 29.9 %copy-start.4 = (s32[2]{0:T(128)S(1)}, s32[2]{0:T(128)}, u32[]{:S(2)}) copy-start(s32[2]{0:T(128)} %ctx_ref.1) | copy-start | bytes 28
  41.8 22.8 %copy-start = (bf16[512,2048]{1,0:T(8,128)(2,1)S(1)}, bf16[512,2048]{1,0:T(8,128)(2,1)}, u32[]{:S(2)}) copy-start(bf16[512,2048]{1,0:T(8,128)(2,1)} %vw_ref.1) | copy-start | bytes 6291460

commit v3 on v2

--- a/solution.py
+++ b/solution.py
@@ -600,7 +600,7 @@
 def decode_kernel(
     lens_ref, owner_ref, ctx_ref, q_ref, new_ref, spans_ref, part_ref, cache_ref,
     out_ref, whole_ref,
-    bufs, sems, whole_sem, m_ref, l_ref, acc_ref,
+    bufs, sems, whole_sem, tools,
     *, lat, heads, steps, blk, depth, scale, rows_local, span_len
 ):
     ranks, owned, block, kv = q_ref.shape
@@ -629,10 +629,16 @@
         length = jnp.where(target > 0, length, ctx_ref[r])
         facts.append((target, first, length))
 
+    counts = []
+    for r in range(owned):
+        _, start, length = facts[r]
+        counts.append((start + length + blk - 1) // blk - start // blk)
+    turns = [(count + 1) // 2 for count in counts]
+
     def copy_of(r, t):
         slot = lax.rem(t, depth)
         target, start, _ = facts[r]
-        at = pl.multiple_of(start // blk * blk + t * blk, blk)
+        at = pl.multiple_of((start // blk + jnp.minimum(t, counts[r] - 1)) * blk, blk)
 
         @pl.when(target > 0)
         def _():
@@ -650,64 +656,139 @@
                 cache_ref.at[r, :, pl.ds(at, blk)], bufs.at[r, slot], sems.at[r, slot]
             ).start()
 
-    counts = []
     for r in range(owned):
-        _, start, length = facts[r]
-        counts.append((start + length + blk - 1) // blk - start // blk)
-    for r in range(owned):
-        for t in range(depth - 1):
-            pl.when(t < counts[r])(functools.partial(copy_of, r, jnp.int32(t)))
+        for t in range(3):
+            copy_of(r, jnp.int32(t))
     newest = new_ref[...].astype(jnp.float32)
-    for r in range(owned):
+    full = tools[0][3].shape[1]
+    tail = lax.broadcasted_iota(jnp.int32, (rows, full - kv), 1)
+    lanes = lax.broadcasted_iota(jnp.int32, (rows, 128), 1)
+    piece = 256
+
+    def request(r, tools):
+        peak_ref, sum_ref, acc_ref, asked, scores, tops, weights, fades = tools
         _, start, length = facts[r]
         base = start // blk * blk
         q = q_ref[:, r].reshape(rows, kv)
+        asked[:, :kv] = q
+        asked[:, kv:] = jnp.where(tail == 0, 1.0, 0.0).astype(jnp.bfloat16)
         fresh = jnp.concatenate(
             [newest[s, r : r + 1] for s in range(steps)]
             + [jnp.zeros((128 - steps, kv), jnp.float32)],
             axis=0,
         ).astype(jnp.bfloat16)
-        s = trans_dot(q, fresh)
-        row_step = (lax.broadcasted_iota(jnp.int32, s.shape, 0) // heads) % steps
-        col = lax.broadcasted_iota(jnp.int32, s.shape, 1)
-        s = jnp.where(col <= row_step, s, NEGATIVE)
-        m = jnp.max(s, axis=1, keepdims=True)
-        w = jnp.exp2((s - m) * scale)
-        l_ref[...] = jnp.broadcast_to(jnp.sum(w, axis=1, keepdims=True), l_ref.shape)
-        m_ref[...] = jnp.broadcast_to(m, m_ref.shape)
-        acc_ref[...] = jnp.dot(
-            w.astype(jnp.bfloat16), fresh[:, :lat], preferred_element_type=jnp.float32
-        )
-
-        def step(t, carry):
+
+        def take(t):
             slot = lax.rem(t, depth)
-            pl.when(t + depth - 1 < counts[r])(lambda: copy_of(r, t + depth - 1))
             pltpu.make_async_copy(
                 cache_ref.at[r, :, pl.ds(0, blk)], bufs.at[r, slot], sems.at[r, slot]
             ).wait()
-            keys = bufs[r, slot]
-            s = jnp.dot(q, keys, preferred_element_type=jnp.float32)
-            place = base + t * blk + lax.broadcasted_iota(jnp.int32, (1, blk), 1)
+
+        def score(t, side, c):
+            slot = lax.rem(t, depth)
+            place = base + t * blk + c * piece + lax.broadcasted_iota(jnp.int32, (16, piece), 1)
             hide = jnp.where((place >= start) & (place < start + length), 0.0, NEGATIVE)
-            s = s + hide
-            old = m_ref[:, :1]
-            new = jnp.maximum(old, jnp.max(s, axis=1, keepdims=True))
-            alpha = jnp.exp2((old - new) * scale)
-            w = jnp.exp2((s - new) * scale)
-            l_new = l_ref[:, :1] * alpha + jnp.sum(w, axis=1, keepdims=True)
-            l_ref[...] = jnp.broadcast_to(l_new, l_ref.shape)
-            m_ref[...] = jnp.broadcast_to(new, m_ref.shape)
-            acc_ref[...] = acc_ref[...] * alpha + trans_dot(w.astype(jnp.bfloat16), keys[:lat])
+            hide = hide.astype(jnp.bfloat16)
+            keys = jnp.concatenate(
+                [bufs[r, slot, :, c * piece : (c + 1) * piece]] + [hide] * ((full - kv) // 16),
+                axis=0,
+            )
+            s = jnp.dot(asked[...], keys, preferred_element_type=jnp.float32)
+            scores[side][:, c * piece : (c + 1) * piece] = s
+            top = jnp.maximum(s[:, :128], s[:, 128:])
+            if c > 0:
+                top = jnp.maximum(top, tops[side][...])
+            tops[side][...] = top
+
+        def settle(side):
+            old = peak_ref[...]
+            new = jnp.maximum(old, jnp.max(tops[side][...], axis=1, keepdims=True))
+            fade = jnp.exp2((old - new) * scale)
+            fades[side][...] = fade
+            peak_ref[...] = new
+            sum_ref[...] = sum_ref[...] * fade
+
+        def soften(side, c):
+            at = slice(c * piece, (c + 1) * piece)
+            new = peak_ref[...]
+            s = scores[side][:, at]
+            left = jnp.exp2((s[:, :128] - new) * scale)
+            right = jnp.exp2((s[:, 128:] - new) * scale)
+            sum_ref[...] = sum_ref[...] + (left + right)
+            weights[side][:, at] = jnp.concatenate([left, right], axis=1).astype(jnp.bfloat16)
+
+        def mix(t, side, c):
+            slot = lax.rem(jnp.maximum(t, 0), depth)
+            at = slice(c * piece, (c + 1) * piece)
+            made = trans_dot(weights[side][...], bufs[r, slot, at, :])
+            fade = fades[side][...]
+            for k in range(piece // 128):
+                columns = slice(c * piece + k * 128, c * piece + (k + 1) * 128)
+                acc_ref[:, columns] = (
+                    acc_ref[:, columns] * fade + made[:, k * 128 : (k + 1) * 128]
+                )
+
+        def begin():
+            s = trans_dot(q, fresh)
+            row_step = (lax.broadcasted_iota(jnp.int32, s.shape, 0) // heads) % steps
+            s = jnp.where(lanes <= row_step, s, NEGATIVE)
+            m = jnp.max(s, axis=1, keepdims=True)
+            w = jnp.exp2((s - m) * scale)
+            sum_ref[...] = w
+            peak_ref[...] = jnp.broadcast_to(m, peak_ref.shape)
+            acc_ref[...] = jnp.dot(
+                w.astype(jnp.bfloat16), fresh[:, :lat], preferred_element_type=jnp.float32
+            )
+            weights[1][...] = jnp.zeros(weights[1].shape, jnp.bfloat16)
+            fades[1][...] = jnp.ones(fades[1].shape, jnp.float32)
+
+        def lead(c):
+            score(jnp.int32(0), 0, c)
+
+        def turn(j, carry):
+            for k in (3, 4):
+                pl.when(2 * j + k <= 2 * turns[r])(functools.partial(copy_of, r, 2 * j + k))
+            take(2 * j + 1)
+            take(2 * j + 2)
+            for side in range(2):
+                t = 2 * j + side
+                settle(side)
+                for c in range(blk // piece):
+                    score(t + 1, 1 - side, c)
+                    soften(side, c)
+                    mix(t - 1, 1 - side, c)
             return carry
 
-        lax.fori_loop(0, counts[r], step, 0)
-        done = (acc_ref[...] / l_ref[:, :1]).astype(out_ref.dtype)
-        for p in range(ranks):
-            out_ref[p, r] = done[p * block : (p + 1) * block]
+        def last(c):
+            mix(2 * turns[r] - 1, 1, c)
+
+        def finish():
+            total = jnp.sum(sum_ref[...], axis=1, keepdims=True)
+            done = (acc_ref[...] * (1.0 / total)).astype(out_ref.dtype)
+            for p in range(ranks):
+                out_ref[p, r] = done[p * block : (p + 1) * block]
+
+        return take, begin, lead, turn, last, finish
+
+    asks = [request(r, tools[r]) for r in range(owned)]
+    for ask in asks:
+        ask[1]()
+    for ask in asks:
+        ask[0](jnp.int32(0))
+    for c in range(blk // piece):
+        for ask in asks:
+            ask[2](c)
+    for r in range(owned):
+        lax.fori_loop(0, turns[r], asks[r][3], 0)
+    for c in range(lat // piece):
+        for ask in asks:
+            ask[4](c)
+    for ask in asks:
+        ask[5]()
     shown.wait()
 
 
-def decode_pallas(lens, owner, ctx, query, newest, spans, part, cache, lat, heads, all_columns, width, rows_local, blk=512, depth=4):
+def decode_pallas(lens, owner, ctx, query, newest, spans, part, cache, lat, heads, all_columns, width, rows_local, blk=512, depth=6):
     ranks, owned, block, kv = query.shape
     rows = ranks * block
     steps = block // heads
@@ -735,9 +816,19 @@
             pltpu.VMEM((owned, depth, kv, blk), jnp.bfloat16),
             pltpu.SemaphoreType.DMA((owned, depth)),
             pltpu.SemaphoreType.DMA((1,)),
-            pltpu.VMEM((rows, 128), jnp.float32),
-            pltpu.VMEM((rows, 128), jnp.float32),
-            pltpu.VMEM((rows, lat), jnp.float32),
+            [
+                [
+                    pltpu.VMEM((rows, 128), jnp.float32),
+                    pltpu.VMEM((rows, 128), jnp.float32),
+                    pltpu.VMEM((rows, lat), jnp.float32),
+                    pltpu.VMEM((rows, -(-(kv + 16) // 128) * 128), jnp.bfloat16),
+                    [pltpu.VMEM((rows, blk), jnp.float32)] * 2,
+                    [pltpu.VMEM((rows, 128), jnp.float32)] * 2,
+                    [pltpu.VMEM((rows, blk), jnp.bfloat16)] * 2,
+                    [pltpu.VMEM((rows, 128), jnp.float32)] * 2,
+                ]
+            ]
+            * owned,
         ],
         compiler_params=pltpu.CompilerParams(vmem_limit_bytes=40 << 20),
         cost_estimate=pl.CostEstimate(

time: 67 us -> 65.6 us (0.979)
  the two profiles are of different devices: /device:TPU:31 before, /device:TPU:0 now
where the time goes in v3:
time: 65.6 us; the launch traced here: 65.9 us
  Pallas kernels  64.3 us (98%)
  between operations  0.87 us (1%)
  local copies, waits for them, and re-layouts  0.69 us (1%)
    pallas_call x1, Pallas kernels, gather_pallas(): pl.pallas_call(functools.partial(gather_kernel, lat=lat, ranks=ranks, hea...  36.4 us
    pallas_call x1, Pallas kernels, return_pallas(): pl.pallas_call(functools.partial(return_kernel, lat=lat, ranks=ranks, loo...  17.9 us
    pallas_call x1, Pallas kernels, decode_pallas(): pl.pallas_call(functools.partial(decode_kernel, lat=lat, heads=heads, ste...  6.86 us
    pallas_call x1, Pallas kernels, project_pallas(): pl.pallas_call(functools.partial(project_kernel, heads=heads, lat=lat), o...  3.13 us

profile of v3, /device:TPU:0, one launch (start us, length us, event | category | flops | bytes accessed | tf_op | source)
XLA Modules:
  0.0 65.9 jit_solution(6604680849187277249)
XLA Ops:
  0.6 0.0 copy-start.3
  0.6 0.7 %copy-done.3 = s32[2,4]{1,0:T(2,128)S(1)} copy-done((s32[2,4]{1,0:T(2,128)S(1)}, s32[2,4]{1,0:T(2,128)}, u32[]{:S(2)}) %copy-start.3) | copy-done | bytes 56
  1.3 0.0 copy-start.1
  1.3 0.0 copy-start.2
  1.3 0.0 copy-start.4
  1.3 36.4 %shard_map.113 = (bf16[16,576,128]{2,1,0:T(8,128)(2,1)S(1)}, bf16[1024,576]{1,0:T(8,128)(2,1)S(1)}, bf16[8,2,32,576]{3,2,1,0:T(8,128)(2,1)S(1)}, bf16[1024,1024]{1,0:T(8,128)(2,1)S(1)}) custom-call(s32[2,4]{1,0:T(2,128)S(1)} %copy-done.3, bf16[576,128]{1,0:T(8,128)(2,1)} %bitcast.9, bf16[512,192]{1,0:T(8,128)(2,1)} %bitcast.8, bf16[512,2048]{1,0:T(8,128)(2,1)} %kw_hbm.3, ...), custom_call_target="tpu_custom_call" | custom-call | flops 12000000000 | bytes 12582912 | tf_op jit(solution)/shard_map/pallas_call | solution.py:558
  37.7 0.0 copy-done.1
  37.7 0.0 copy-done.2
  37.8 0.0 copy-done.4
  37.8 6.9 %shard_map.114 = (bf16[8,2,32,512]{3,2,1,0:T(8,128)(2,1)S(1)}, bf16[1024,2048]{1,0:T(8,128)(2,1)}) custom-call(s32[2,4]{1,0:T(2,128)S(1)} %copy-done.3, s32[2,4]{1,0:T(2,128)S(1)} %copy-done.2, s32[2]{0:T(128)S(1)} %copy-done.4, bf16[8,2,32,576]{3,2,1,0:T(8,128)(2,1)S(1)} %get-tuple-element.14.q_ref, bf16[2,2,576]{2,1,0:T(2,128)(2,1)S(1)} %copy-done.1, ...), custom_call_target="tpu_custom_call" | custom-call | flops 5000000000 | bytes 10485760 | tf_op jit(solution)/shard_map/pallas_call | solution.py:796
  44.6 0.0 copy-start
  44.6 17.9 %shard_map.115 = (bf16[8,2,32,512]{3,2,1,0:T(8,128)(2,1)S(1)}, bf16[1024,1024]{1,0:T(8,128)(2,1)S(1)}) custom-call(s32[2,4]{1,0:T(2,128)S(1)} %copy-done.3, bf16[1024,576]{1,0:T(8,128)(2,1)S(1)} %get-tuple-element.12.rows_ref, bf16[16,576,128]{2,1,0:T(8,128)(2,1)S(1)} %get-tuple-element.13.spans_ref, bf16[8,2,32,512]{3,2,1,0:T(8,128)(2,1)S(1)} %get-tuple-element.16.lo_ref, ...), custom_call_target="tpu_custom_call" | custom-call | flops 12000000000 | bytes 12582912 | tf_op jit(solution)/shard_map/pallas_call | solution.py:903
  62.6 0.0 copy-done
  62.6 3.1 %shard_map.116 = (bf16[32,2048]{1,0:T(8,128)(2,1)}, bf16[1024,2048]{1,0:T(8,128)(2,1)}) custom-call(bf16[8,2,32,512]{3,2,1,0:T(8,128)(2,1)S(1)} %get-tuple-element.17.back_ref, bf16[512,2048]{1,0:T(8,128)(2,1)S(1)} %copy-done, bf16[1024,1024]{1,0:T(8,128)(2,1)S(1)} %get-tuple-element.18.part_ref, ...), custom_call_target="tpu_custom_call", output_to_operand_aliasing={{1}: (3, {})} | custom-call | tf_op jit(solution)/shard_map/pallas_call | solution.py:975
Async XLA Ops:
  0.6 0.7 %copy-start.3 = (s32[2,4]{1,0:T(2,128)S(1)}, s32[2,4]{1,0:T(2,128)}, u32[]{:S(2)}) copy-start(s32[2,4]{1,0:T(2,128)} %lens_ref.5) | copy-start | bytes 100
  1.3 36.4 %copy-start.1 = (bf16[2,2,576]{2,1,0:T(2,128)(2,1)S(1)}, bf16[2,2,576]{2,1,0:T(2,128)(2,1)}, u32[]{:S(2)}) copy-start(bf16[2,2,576]{2,1,0:T(2,128)(2,1)} %new_ref.1) | copy-start | bytes 13828
  1.3 36.4 %copy-start.2 = (s32[2,4]{1,0:T(2,128)S(1)}, s32[2,4]{1,0:T(2,128)}, u32[]{:S(2)}) copy-start(s32[2,4]{1,0:T(2,128)} %owner_ref.1) | copy-start | bytes 100
  1.3 36.4 %copy-start.4 = (s32[2]{0:T(128)S(1)}, s32[2]{0:T(128)}, u32[]{:S(2)}) copy-start(s32[2]{0:T(128)} %ctx_ref.1) | copy-start | bytes 28
  44.6 18.0 %copy-start = (bf16[512,2048]{1,0:T(8,128)(2,1)S(1)}, bf16[512,2048]{1,0:T(8,128)(2,1)}, u32[]{:S(2)}) copy-start(bf16[512,2048]{1,0:T(8,128)(2,1)} %vw_ref.1) | copy-start | bytes 6291460
